TPU v7x, 8 devices: a whole 2x2x1 slice. The times are simulated.
8 devices in a mesh: graphs: 2 (over z, y), nodes: 4 (over x, core).
Axes of the slice: x: 2, y: 2, z: 1, core: 2. Of those that a mesh axis runs over, the one named last changes fastest.
Arguments:
- x_feat: bfloat16 [8192, 512], P(('graphs', 'nodes')), parts along dimension 0
- valid: int32 [8192], P(('graphs', 'nodes')), parts along dimension 0
- halo_slot: int32 [8, 4, 32], P(('graphs', 'nodes')), parts along dimension 0
- edge_src: int32 [8, 14336], P(('graphs', 'nodes')), parts along dimension 0
- edge_dst: int32 [8, 14336], P(('graphs', 'nodes')), parts along dimension 0
- edge_mask: int32 [8, 14336], P(('graphs', 'nodes')), parts along dimension 0
- bal_perm: int32 [8192], P(('graphs', 'nodes')), parts along dimension 0
- pos_enc: bfloat16 [8192, 512], P(('graphs', 'nodes')), parts along dimension 0
- y_cot: bfloat16 [8192, 512], P(('graphs', 'nodes')), parts along dimension 0
- w_msg: bfloat16 [512, 512], replicated
- w_self: bfloat16 [512, 512], replicated
- w_q: bfloat16 [512, 512], replicated
- w_k: bfloat16 [512, 64], replicated
- w_v: bfloat16 [512, 64], replicated
- w_o: bfloat16 [512, 512], replicated
- w_up: bfloat16 [512, 2048], replicated
- w_down: bfloat16 [2048, 512], replicated
Outputs:
- output 1: bfloat16 [8192, 512], P(('graphs', 'nodes')), parts along dimension 0
- output 2: bfloat16 [8192, 512], P(('graphs', 'nodes')), parts along dimension 0
- output 3: float32 [1024, 512], P('graphs'), parts along dimension 0
- output 4: float32 [1024, 512], P('graphs'), parts along dimension 0
- output 5: float32 [1024, 512], P('graphs'), parts along dimension 0
- output 6: float32 [1024, 64], P('graphs'), parts along dimension 0
- output 7: float32 [1024, 64], P('graphs'), parts along dimension 0
- output 8: float32 [1024, 512], P('graphs'), parts along dimension 0
- output 9: float32 [1024, 2048], P('graphs'), parts along dimension 0
- output 10: float32 [4096, 512], P('graphs'), parts along dimension 0
There are 2 independent parts. A program takes and returns all parts, laid end to end along the dimension named above; an argument that names none is the same for every part.
All inputs are finite; a program needn't handle non-finite values.
Results may differ from a plain program's by a relative error of at most 0.02.
Values are sent between devices in bfloat16 or wider.
A program may use at most 1 GiB of HBM per device.

v0:
```python
import functools
import math

import jax
import jax.numpy as jnp
from jax import lax
from jax.experimental import pallas as pl
from jax.experimental.pallas import tpu as pltpu
from jax.sharding import PartitionSpec as P

NEG_FILL = -1e30
LOG2E = math.log2(math.e)
TAIL = 32
F32 = jnp.float32
BF16 = jnp.bfloat16
NN = (((1,), (0,)), ((), ()))
NT = (((1,), (1,)), ((), ()))
TN = (((0,), (0,)), ((), ()))
TT = (((0,), (1,)), ((), ()))


def dot(a, b, dims=NN):
    return lax.dot_general(a, b, dims, preferred_element_type=F32)


def remote(src, dst, send, recv, peer):
    return pltpu.make_async_remote_copy(src_ref=src, dst_ref=dst, send_sem=send, recv_sem=recv, device_id={'nodes': peer}, device_id_type=pl.DeviceIdType.MESH)


def neighbours():
    me = lax.axis_index('nodes')
    chip, side = me // 2, lax.rem(me, 2)
    return me, chip, side, chip * 2 + 1 - side, (1 - chip) * 2 + side, (1 - chip) * 2 + 1 - side


def meet(peers):
    barrier = pltpu.get_barrier_semaphore()
    for peer in peers:
        pl.semaphore_signal(barrier, inc=1, device_id={'nodes': peer}, device_id_type=pl.DeviceIdType.MESH)
    pl.semaphore_wait(barrier, len(peers))


CHUNKS, EDGE_STEP, POS_PIECES, KV_PIECES = 4, 512, 4, 2


def front_kernel(meta_ref, x_ref, pos_ref, src_ref, dst_ref, on_ref, w_qt_ref, w_kv_ref, w_msg_ref, w_self_ref, q_ref, kv_ref, kvt_ref, hid_ref, agg_ref, pre_ref, adj_ref, slot_ref, count_ref, meta_all, pos_all, pos_acc, counts_acc, edge_acc, halo_out, halo_in, kv_all, meta_send, meta_recv, pos_send, pos_recv, halo_send, halo_recv, kv_send, kv_recv):
    rows_dev, width = x_ref.shape
    table_rows = adj_ref.shape[0]
    half = rows_dev // 2
    nodes = meta_all.shape[0]
    halo_pair = halo_in.shape[1]
    me, chip, side, mate, cross, other = neighbours()
    peers = (mate, cross, other)
    meet(peers)

    meta_copies = [remote(meta_ref, meta_all.at[me], meta_send.at[i], meta_recv.at[me], peer) for i, peer in enumerate(peers)]
    for copy in meta_copies:
        copy.start()
    piece = rows_dev // POS_PIECES

    def pos_rows(index):
        return pl.ds(index * piece, piece)

    pos_to_cross = [remote(pos_ref.at[pos_rows(k), :], pos_all.at[me, pos_rows(k), :], pos_send.at[0, k], pos_recv.at[0, k], cross) for k in range(POS_PIECES)]
    pos_to_mate = [remote(pos_ref.at[pos_rows(k), :], pos_all.at[me, pos_rows(k), :], pos_send.at[1, k], pos_recv.at[1, k], mate) for k in range(POS_PIECES)]
    pos_relay = [remote(pos_all.at[cross, pos_rows(k), :], pos_all.at[cross, pos_rows(k), :], pos_send.at[2, k], pos_recv.at[2, k], mate) for k in range(POS_PIECES)]
    for copy in pos_to_cross + pos_to_mate:
        copy.start()
    meta_all[me] = meta_ref[...]

    def relay_pos(k):
        pos_to_cross[k].wait_recv()
        pos_relay[k].start()

    def place_pos(owner, source, first):
        perm = meta_all[owner, 0:1, :] - me * rows_dev
        size = 256

        def body(index, carry):
            rows = pl.ds(pl.multiple_of(index * size, size), size)
            hot = jnp.where(index * size + lax.broadcasted_iota(jnp.int32, (size, rows_dev), 0) == perm, 1.0, 0.0).astype(BF16)
            part = dot(hot, source[...])
            pos_acc[rows, :] = part if first else pos_acc[rows, :] + part
            return carry

        lax.fori_loop(0, rows_dev // size, body, 0)

    edges = src_ref.shape[1]
    steps = edges // (CHUNKS * EDGE_STEP)
    assert CHUNKS * EDGE_STEP * steps == edges and EDGE_STEP * steps < 4096

    def edge_block(index):
        cols = pl.ds(pl.multiple_of(index * EDGE_STEP, EDGE_STEP), EDGE_STEP)
        src, dst, on = src_ref[:, cols], dst_ref[:, cols], on_ref[:, cols]
        upper = dst >= half
        place = jnp.where(upper, dst - half, dst)
        weight = jnp.where(on > 0, jnp.where(upper, 4096.0, 1.0), 0.0)
        src_hot = jnp.where(lax.broadcasted_iota(jnp.int32, (table_rows, EDGE_STEP), 0) == src, 1.0, 0.0).astype(BF16)
        dst_hot = jnp.where(lax.broadcasted_iota(jnp.int32, (half, EDGE_STEP), 0) == place, weight, 0.0).astype(BF16)
        return dot(src_hot, dst_hot, NT)

    def count_chunk(chunk):
        edge_acc[...] = jnp.zeros_like(edge_acc)

        def body(step, carry):
            edge_acc[...] += edge_block(chunk * steps + step)
            return carry

        lax.fori_loop(0, steps, body, 0)
        total = edge_acc[...]
        high = jnp.floor(total * (1.0 / 4096.0))
        low = total - high * 4096.0
        if chunk == 0:
            counts_acc[:, :half] = low
            counts_acc[:, half:] = high
        elif chunk < CHUNKS - 1:
            counts_acc[:, :half] += low
            counts_acc[:, half:] += high
        else:
            adj_ref[:, :half] = (counts_acc[:, :half] + low).astype(BF16)
            adj_ref[:, half:] = (counts_acc[:, half:] + high).astype(BF16)

    def halo_copy(peer, owner):
        return remote(halo_out.at[peer], halo_in.at[owner], halo_send.at[peer], halo_recv.at[owner], peer)

    count_chunk(0)
    for peer in peers:
        remote(meta_ref, meta_all.at[peer], meta_send.at[0], meta_recv.at[peer], peer).wait_recv()
    tables = meta_all[0, :, 0:nodes * halo_pair]
    for node in range(1, nodes):
        tables = jnp.maximum(tables, meta_all[node, :, 0:nodes * halo_pair])
    tables = jnp.where(lax.broadcasted_iota(jnp.int32, tables.shape, 0) == 2 + me, tables, -1)
    slots = jnp.max(tables.astype(F32), axis=0, keepdims=True).astype(jnp.int32)
    slot_ref[...] = slots
    slot_hot = jnp.where(lax.broadcasted_iota(jnp.int32, (rows_dev, nodes * halo_pair), 0) == slots, 1.0, 0.0).astype(BF16)
    halo_out[...] = dot(slot_hot, x_ref[...], TN).astype(BF16).reshape(halo_out.shape)
    relay_pos(0)
    place_pos(me, pos_ref, True)
    for peer in peers:
        halo_copy(peer, me).start()
    halo_in[me] = halo_out[me]
    for node in range(nodes):
        held = jnp.sum(meta_all[node, 1:2, :].astype(F32), axis=1, keepdims=True).astype(jnp.int32)
        count_ref[node:node + 1, :] = jnp.broadcast_to(held, (1, count_ref.shape[1]))
    count_chunk(1)
    relay_pos(1)
    for copy in pos_to_mate:
        copy.wait_recv()
    place_pos(mate, pos_all.at[mate], False)
    count_chunk(2)
    relay_pos(2)
    count_chunk(3)
    relay_pos(3)
    place_pos(cross, pos_all.at[cross], False)
    for copy in pos_relay:
        copy.wait_recv()
    place_pos(other, pos_all.at[other], False)

    hidden = (x_ref[...].astype(F32) + pos_acc[...]).astype(BF16)
    hid_ref[...] = hidden
    kv_all[me] = dot(hidden, w_kv_ref[...]).astype(BF16)
    q_ref[...] = dot(w_qt_ref[...], hid_ref[...], NT).astype(BF16)
    kv_piece = rows_dev // KV_PIECES

    def kv_copy(owner, k, kind, peer):
        rows = pl.ds(k * kv_piece, kv_piece)
        return remote(kv_all.at[owner, rows, :], kv_all.at[owner, rows, :], kv_send.at[kind, k], kv_recv.at[kind, k], peer)

    kv_to_cross = [kv_copy(me, k, 0, cross) for k in range(KV_PIECES)]
    kv_to_mate = [kv_copy(me, k, 1, mate) for k in range(KV_PIECES)]
    kv_relay = [kv_copy(cross, k, 2, mate) for k in range(KV_PIECES)]
    for copy in kv_to_cross + kv_to_mate:
        copy.start()
    size = 2 * w_qt_ref.shape[0] // 8
    eye = jnp.where(lax.broadcasted_iota(jnp.int32, (size, size), 0) == lax.broadcasted_iota(jnp.int32, (size, size), 1), 1.0, 0.0).astype(BF16)

    def keep_kv(owner):
        rows = pl.ds(pl.multiple_of(owner * rows_dev, rows_dev), rows_dev)
        kv_ref[rows, :] = kv_all[owner]
        kvt_ref[:, rows] = dot(eye, kv_all[owner], NT).astype(BF16)

    for peer in peers:
        halo_copy(me, peer).wait_recv()
    agg = dot(adj_ref[:rows_dev, :], x_ref[...], TN) + dot(adj_ref[rows_dev:, :], halo_in[...].reshape(nodes * halo_pair, width), TN)
    agg_ref[...] = agg.astype(BF16)
    keep_kv(me)
    kv_to_cross[0].wait_recv()
    kv_relay[0].start()
    pre_ref[...] = dot(agg_ref[...], w_msg_ref[...]) + dot(x_ref[...], w_self_ref[...])
    for k in range(1, KV_PIECES):
        kv_to_cross[k].wait_recv()
        kv_relay[k].start()
    for copy in kv_to_mate:
        copy.wait_recv()
    keep_kv(mate)
    keep_kv(cross)
    for copy in kv_relay:
        copy.wait_recv()
    keep_kv(other)
    for copy in meta_copies + pos_to_cross + pos_to_mate + pos_relay + [halo_copy(peer, me) for peer in peers] + kv_to_cross + kv_to_mate + kv_relay:
        copy.wait_send()


def front(meta, x_feat, pos_enc, edge_src, edge_dst, edge_mask, w_q_t, w_kv, w_msg, w_self, nodes, halo_pair):
    rows, width = x_feat.shape
    pair = w_kv.shape[1]
    keys = nodes * rows
    table_rows = rows + nodes * halo_pair
    vmem = pl.BlockSpec(memory_space=pltpu.VMEM)
    dma = pltpu.SemaphoreType.DMA
    out = [((width, rows), BF16), ((keys, pair), BF16), ((pair, keys), BF16), ((rows, width), BF16), ((rows, width), BF16), ((rows, width), F32), ((table_rows, rows), BF16), ((1, nodes * halo_pair), jnp.int32), ((nodes, 512), jnp.int32)]
    return pl.pallas_call(
        front_kernel,
        out_shape=[jax.ShapeDtypeStruct(shape, dtype) for shape, dtype in out],
        in_specs=[vmem] * 10,
        out_specs=[vmem] * len(out),
        scratch_shapes=[
            pltpu.VMEM((nodes,) + meta.shape, jnp.int32),
            pltpu.VMEM((nodes, rows, width), BF16),
            pltpu.VMEM((rows, width), F32),
            pltpu.VMEM((table_rows, rows), F32),
            pltpu.VMEM((table_rows, rows // 2), F32),
            pltpu.VMEM((nodes, halo_pair, width), BF16),
            pltpu.VMEM((nodes, halo_pair, width), BF16),
            pltpu.VMEM((nodes, rows, pair), BF16),
            dma((3,)), dma((nodes,)), dma((3, POS_PIECES)), dma((3, POS_PIECES)), dma((nodes,)), dma((nodes,)), dma((3, KV_PIECES)), dma((3, KV_PIECES)),
        ],
        compiler_params=pltpu.CompilerParams(vmem_limit_bytes=52 << 20, collective_id=2, has_side_effects=True),
        cost_estimate=pl.CostEstimate(flops=24 << 30, bytes_accessed=20 << 20, transcendentals=0),
        name='front',
    )(meta, x_feat, pos_enc, edge_src, edge_dst, edge_mask, w_q_t, w_kv, w_msg, w_self)


def mask_tail(scores, chunk, key_chunk, part_rows, count_ref):
    start = chunk * key_chunk
    part = start // part_rows
    first = start - part * part_rows + key_chunk - TAIL
    row_ix = first + lax.broadcasted_iota(jnp.int32, (TAIL, scores.shape[1]), 0)
    tail = jnp.where(row_ix < count_ref[pl.ds(part, 1), :scores.shape[1]], scores[key_chunk - TAIL:, :], NEG_FILL)
    return jnp.concatenate([scores[:key_chunk - TAIL, :], tail], axis=0)


def attention_fwd_kernel(head_dim, q_block, key_chunk, part_rows, count_ref, q_ref, kv_ref, kvt_ref, out_ref, lse_ref, w_q, s_buf, stat):
    heads = q_ref.shape[0] // head_dim
    blocks = q_ref.shape[1] // q_block
    units = heads * blocks
    keys = kv_ref.shape[0]
    chunks = keys // key_chunk
    factor = head_dim ** -0.5 * LOG2E
    groups = key_chunk // 8

    def load_weights(unit):
        head, block = unit // blocks, lax.rem(unit, blocks)
        w_q[:head_dim, :] = q_ref[pl.ds(pl.multiple_of(head * head_dim, head_dim), head_dim), pl.ds(pl.multiple_of(block * q_block, q_block), q_block)]

    def score_stage(slot, chunk, run_max):
        rows = pl.ds(pl.multiple_of(chunk * key_chunk, key_chunk), key_chunk)
        scores = mask_tail(dot(kv_ref[rows, :], w_q[...]), chunk, key_chunk, part_rows, count_ref)
        s_buf[slot, rows, :] = scores
        return jnp.maximum(run_max, jnp.max(scores.reshape(groups, 8, q_block), axis=0))

    w_q[head_dim:, :] = jnp.zeros((w_q.shape[0] - head_dim, q_block), BF16)
    floor = jnp.full((8, q_block), -jnp.inf, F32)
    load_weights(0)
    stat[...] = lax.fori_loop(0, chunks, lambda chunk, run_max: score_stage(0, chunk, run_max), floor)

    def unit_body(unit, carry):
        slot = lax.rem(unit, 2)
        load_weights(jnp.minimum(unit + 1, units - 1))
        top = jnp.max(stat[...], axis=0, keepdims=True) * factor

        def chunk_body(chunk, state):
            run_max, run_sum, weighted = state
            cols = pl.ds(pl.multiple_of(chunk * key_chunk, key_chunk), key_chunk)
            prob = jnp.exp2(s_buf[slot, cols, :] * factor - top)
            run_sum = run_sum + jnp.sum(prob.reshape(groups, 8, q_block), axis=0)
            weighted = weighted + dot(kvt_ref[head_dim:2 * head_dim, cols], prob.astype(BF16))
            return score_stage(1 - slot, chunk, run_max), run_sum, weighted

        run_max, run_sum, weighted = lax.fori_loop(0, chunks, chunk_body, (floor, jnp.zeros((8, q_block), F32), jnp.zeros((head_dim, q_block), F32)))
        stat[...] = run_max
        total = jnp.sum(run_sum, axis=0, keepdims=True)
        head, block = unit // blocks, lax.rem(unit, blocks)
        cols = pl.ds(pl.multiple_of(block * q_block, q_block), q_block)
        out_ref[pl.ds(pl.multiple_of(head * head_dim, head_dim), head_dim), cols] = (weighted / total).astype(BF16)
        lse_ref[pl.ds(head, 1), cols] = top + jnp.log2(total)
        return carry

    lax.fori_loop(0, units, unit_body, 0)


def attention_forward(counts, q_t, kv, kv_t, head_dim, part_rows):
    width, rows = q_t.shape
    keys = kv.shape[0]
    heads = width // head_dim
    q_block, key_chunk = 256, 1024
    vmem = pl.BlockSpec(memory_space=pltpu.VMEM)
    return pl.pallas_call(
        functools.partial(attention_fwd_kernel, head_dim, q_block, key_chunk, part_rows),
        out_shape=[jax.ShapeDtypeStruct((width, rows), BF16), jax.ShapeDtypeStruct((heads, rows), F32)],
        in_specs=[vmem] * 4,
        out_specs=[vmem, vmem],
        scratch_shapes=[pltpu.VMEM((2 * head_dim, q_block), BF16), pltpu.VMEM((2, keys, q_block), F32), pltpu.VMEM((8, q_block), F32)],
        compiler_params=pltpu.CompilerParams(vmem_limit_bytes=48 << 20),
        cost_estimate=pl.CostEstimate(flops=4 * heads * rows * keys * head_dim, bytes_accessed=4 << 20, transcendentals=heads * rows * keys),
        name='attention_fwd',
    )(counts, q_t, kv, kv_t)


FINAL_STEPS, FINAL_LAG = 14, 2
FIRST_PIECES, HOLD_PIECES, HOLD_STEP = 2, 7, 68


def backward_kernel(head_dim, q_block, key_chunk, part_rows, pieces, count_ref, q_ref, do_ref, o_ref, lse_ref, kv_ref, kvt_ref, hid_ref, x_ref, agg_ref, dz_ref, dpre_ref, adj_ref, slot_ref, w_msg_ref, w_self_ref, w_qt_ref, w_kv_ref, up_ref, down_ref, *rest):
    arrays = len(pieces)
    dx_ref, rest = rest[0], rest[1:]
    sum_refs, rest = rest[:arrays], rest[arrays:]
    kv_sum_ref, rest = rest[0], rest[1:]
    w_q, w_do, lse_buf, delta_buf, p_buf, ds_buf, dq_acc, dq_all, dkv_acc, dkv_in, dkv_sum, local, own, from_mate, from_cross, kv_local, kv_own, kv_in, halo_out, halo_in, dx_acc, own_sem, send_sem, recv_sem, dkv_send, dkv_recv, kv_sem, kv_send, kv_recv, halo_send, halo_recv = rest
    heads = q_ref.shape[0] // head_dim
    blocks = q_ref.shape[1] // q_block
    units = heads * blocks
    chunks = kv_ref.shape[0] // key_chunk
    steps = units * chunks
    per_group = steps // 4
    halves = part_rows // key_chunk
    scale = head_dim ** -0.5
    factor = scale * LOG2E
    total = own.shape[0]
    first_small = total - 4
    half_rows, width = own.shape[1:]

    me, chip, side, mate, cross, other = neighbours()

    spots = [(array, j) for array in range(arrays) for j in range(pieces[array])]

    def block(refs, spot, half):
        array, j = spot
        ref = refs[array]
        if ref.shape[1] > width:
            return ref.at[pl.ds(half * half_rows, half_rows), pl.ds(j * width, width)]
        return ref.at[pl.ds((half * pieces[array] + j) * half_rows, half_rows), :]

    def source(index, half):
        if index < first_small:
            return block((up_ref, down_ref), spots[index], half)
        return local.at[index - first_small, pl.ds(half * half_rows, half_rows), :]

    def to_peer(src, dst, kind, index, peer):
        return remote(src, dst, send_sem.at[kind, index], recv_sem.at[kind, index], peer)

    def mate_copy(index):
        return to_peer(source(index, 1 - side), from_mate.at[index], 0, index, mate)

    def own_copy(index):
        return pltpu.make_async_copy(source(index, side), own.at[index], own_sem.at[0, index])

    def cross_copy(index):
        return to_peer(own.at[index], from_cross.at[index], 1, index, cross)

    def back_copy(index, half):
        return to_peer(from_mate.at[index], block(sum_refs, spots[index], half), 2, index, mate)

    def keep_copy(index):
        return pltpu.make_async_copy(from_mate.at[index], block(sum_refs, spots[index], side), own_sem.at[1, index])

    def chip_sum(index):
        to_peer(own.at[index], from_mate.at[index], 0, index, mate).wait_recv()
        pltpu.make_async_copy(own.at[index], own.at[index], own_sem.at[0, index]).wait()
        own[index] = own[index] + from_mate[index]

    def group_sum(index):
        cross_copy(index).wait_recv()
        from_mate[index] = own[index] + from_cross[index]

    def start_out(index):
        keep_copy(index).start()
        back_copy(index, side).start()

    dkv_copies = [remote(src, dkv_in.at[i], dkv_send.at[i], dkv_recv.at[i], peer) for i, (src, peer) in enumerate(((dkv_acc.at[0], mate), (dkv_sum, cross), (dkv_acc.at[2], mate)))]

    def kv_rows(half):
        return pl.ds(half * half_rows, half_rows)

    kv_to_mate = remote(kv_local.at[kv_rows(1 - side), :], kv_in.at[0], kv_send.at[0], kv_recv.at[0], mate)
    kv_to_cross = remote(kv_own.at[0], kv_in.at[1], kv_send.at[1], kv_recv.at[1], cross)
    kv_keep = pltpu.make_async_copy(kv_own.at[1], kv_sum_ref.at[kv_rows(side), :], kv_sem)

    def kv_back(half):
        return remote(kv_own.at[1], kv_sum_ref.at[kv_rows(half), :], kv_send.at[2], kv_recv.at[2], mate)

    halo_pair = halo_out.shape[1]

    def halo_copy(peer, owner):
        return remote(halo_out.at[peer], halo_in.at[owner], halo_send.at[peer], halo_recv.at[owner], peer)

    meet((mate, cross, other))
    for index in range(first_small):
        mate_copy(index).start()
        own_copy(index).start()

    def unit_spots(unit):
        head, place = unit // blocks, lax.rem(unit, blocks)
        return head, pl.ds(pl.multiple_of(head * head_dim, head_dim), head_dim), pl.ds(pl.multiple_of(place * q_block, q_block), q_block)

    def prepare(unit, carry):
        head, rows, cols = unit_spots(unit)
        delta_buf[unit] = jnp.sum(do_ref[rows, cols].astype(F32) * o_ref[rows, cols].astype(F32), axis=0, keepdims=True)
        lse_buf[unit] = lse_ref[pl.ds(head, 1), cols]
        dq_acc[unit] = jnp.zeros((head_dim, q_block), F32)
        return carry

    lax.fori_loop(0, units, prepare, 0)
    for index in range(FIRST_PIECES):
        chip_sum(index)
    for slot in range(2):
        w_q[slot, head_dim:, :] = jnp.zeros((head_dim, q_block), BF16)
        w_do[slot, :head_dim, :] = jnp.zeros((head_dim, q_block), BF16)
    dkv_acc[...] = jnp.zeros_like(dkv_acc)
    for index in range(FIRST_PIECES):
        cross_copy(index).start()

    d_agg = dot(dpre_ref[...], w_msg_ref[...], NT).astype(BF16)
    halo_out[...] = dot(adj_ref[part_rows:, :], d_agg).astype(BF16).reshape(halo_out.shape)
    dx_acc[...] = 2.0 * dz_ref[...].astype(F32) + dot(dpre_ref[...], w_self_ref[...], NT)
    dx_acc[...] += dot(adj_ref[:part_rows, :], d_agg)
    for peer in (mate, cross, other):
        halo_copy(peer, me).start()
    halo_in[me] = halo_out[me]
    local[0] = dot(x_ref[...], dpre_ref[...], TN)
    local[1] = dot(agg_ref[...], dpre_ref[...], TN)
    local[2] = dot(o_ref[...], dz_ref[...])

    def place_of(step):
        group = step // per_group
        chunk = step // units
        owner = lax.rem(chip + 1 - group // 2, 2) * 2 + lax.rem(side + 1 - lax.rem(group, 2), 2)
        offset = lax.rem(chunk, halves) * key_chunk
        rows = pl.ds(pl.multiple_of(owner * part_rows + offset, key_chunk), key_chunk)
        return group, owner, offset, rows, lax.rem(step, units), lax.rem(step, 2)

    def first_stage(step):
        group, owner, offset, rows, unit, slot = place_of(step)
        head, unit_rows, cols = unit_spots(unit)
        w_q[slot, :head_dim, :] = q_ref[unit_rows, cols]
        w_do[slot, head_dim:, :] = do_ref[unit_rows, cols]
        kv = kv_ref[rows, :]
        scores = dot(kv, w_q[slot])
        row_ix = offset + key_chunk - TAIL + lax.broadcasted_iota(jnp.int32, (TAIL, q_block), 0)
        tail = jnp.where(row_ix < count_ref[pl.ds(owner, 1), :q_block], scores[key_chunk - TAIL:, :], NEG_FILL)
        scores = jnp.concatenate([scores[:key_chunk - TAIL, :], tail], axis=0)
        prob = jnp.exp2(scores * factor - lse_buf[unit])
        p_buf[slot] = prob.astype(BF16)
        ds_buf[slot] = (prob * (dot(kv, w_do[slot]) - delta_buf[unit])).astype(BF16)

    def second_stage(step):
        group, owner, offset, rows, unit, slot = place_of(step)
        d_scores = ds_buf[slot]
        spot = pl.ds(pl.multiple_of(offset, key_chunk), key_chunk)
        dkv_acc[group, spot, :] += dot(d_scores, w_q[slot], NT) + dot(p_buf[slot], w_do[slot], NT)
        dq_acc[unit] += dot(kvt_ref[:head_dim, rows], d_scores)

    def exchange(step):
        early = jnp.where(step < 4 * (HOLD_PIECES - FIRST_PIECES), 1, 0)
        late = jnp.where(jnp.logical_and(step >= HOLD_STEP, step < HOLD_STEP + 4 * (first_small + 3 - HOLD_PIECES)), 1, 0)
        turn = step // 4 + FIRST_PIECES - late * (HOLD_STEP // 4 + FIRST_PIECES - HOLD_PIECES)
        phase = lax.rem(step, 4)

        @pl.when(jnp.logical_and(early + late == 1, phase == 1))
        def sum_chip():
            chip_sum(turn)

        @pl.when(jnp.logical_and(early + late == 1, phase == 2))
        def send_cross():
            cross_copy(turn).start()

        lap, beat = step // FINAL_STEPS - FINAL_LAG, lax.rem(step, FINAL_STEPS)

        @pl.when(jnp.logical_and(lap >= 0, beat == 0))
        def sum_group():
            group_sum(lap)

        @pl.when(jnp.logical_and(lap >= 0, beat == 1))
        def send_back():
            for k in range(done):
                @pl.when(lap == k)
                def start_piece(k=k):
                    start_out(k)

        @pl.when(step == 3)
        def small_pieces():
            for index in range(first_small, total - 1):
                mate_copy(index).start()
                own_copy(index).start()

        @pl.when(step == per_group + 1)
        def first_group():
            dkv_copies[0].start()

        @pl.when(step == 2 * per_group + 1)
        def second_group():
            dkv_copies[0].wait_recv()
            dkv_sum[...] = dkv_acc[1] + dkv_in[0]

        @pl.when(step == 2 * per_group + 2)
        def send_second():
            dkv_copies[1].start()

        @pl.when(step == 3 * per_group + 1)
        def third_group():
            dkv_copies[2].start()

    done = (steps - 1) // FINAL_STEPS - FINAL_LAG + 1
    assert (steps - 1) % FINAL_STEPS >= 1 and 0 < done <= first_small and HOLD_STEP > 2 * per_group + 2 and HOLD_STEP % 4 == 0

    first_stage(0)

    def body(step, carry):
        exchange(step)
        second_stage(step - 1)
        first_stage(step)
        return carry

    lax.fori_loop(1, steps, body, 0)
    second_stage(steps - 1)

    def gather_dq(unit, carry):
        head, rows, cols = unit_spots(unit)
        dq_all[rows, cols] = (dq_acc[unit] * scale).astype(BF16)
        return carry

    lax.fori_loop(0, units, gather_dq, 0)
    last = total - 1
    local[3] = dot(dq_all[...], hid_ref[...]).T
    dkv_copies[2].wait_recv()
    dkv_copies[1].wait_recv()
    dkv = dkv_acc[3] + dkv_in[2] + dkv_in[1]
    lane = lax.broadcasted_iota(jnp.int32, dkv.shape, 1)
    dkv = jnp.where(lane < head_dim, dkv * scale, dkv).astype(BF16)
    mate_copy(last).start()
    own_copy(last).start()
    kv_local[...] = dot(hid_ref[...], dkv, TN)
    dx_acc[...] += dot(dkv, w_kv_ref[...], NT)
    kv_to_mate.start()
    chip_sum(last)
    kv_to_mate.wait_recv()
    kv_own[0] = kv_local[kv_rows(side), :] + kv_in[0]
    for peer in (mate, cross, other):
        halo_copy(me, peer).wait_recv()
    slot_hot = jnp.where(lax.broadcasted_iota(jnp.int32, (part_rows, 4 * halo_pair), 0) == slot_ref[...], 1.0, 0.0).astype(BF16)
    dx_acc[...] += dot(slot_hot, halo_in[...].reshape(4 * halo_pair, width))
    cross_copy(last).start()
    kv_to_cross.start()
    dx_ref[...] = (dx_acc[...] + dot(dq_all[...], w_qt_ref[...], TN)).astype(BF16)
    for index in range(done, total):
        group_sum(index)
        if index > done:
            start_out(index - 1)
    kv_to_cross.wait_recv()
    kv_own[1] = kv_own[0] + kv_in[1]
    start_out(last)
    kv_keep.start()
    kv_back(side).start()
    for copy in dkv_copies + [kv_to_mate, kv_to_cross, kv_back(side)] + [halo_copy(peer, me) for peer in (mate, cross, other)]:
        copy.wait_send()
    kv_keep.wait()
    kv_back(1 - side).wait_recv()
    for index in range(total):
        mate_copy(index).wait_send()
        cross_copy(index).wait_send()
        keep_copy(index).wait()
        back_copy(index, side).wait_send()
        back_copy(index, 1 - side).wait_recv()


def backward(counts, q_t, do_t, o_t, lse, kv, kv_t, hidden_in, x_feat, agg_msg, d_z, d_pre, adjacency_t, halo_got, w_msg, w_self, w_q_t, w_kv, grad_up, grad_down):
    width, rows = q_t.shape
    keys = kv.shape[0]
    head_dim = kv.shape[1] // 2
    heads = width // head_dim
    nodes = keys // rows
    q_block, key_chunk = 512, 512
    units = heads * rows // q_block
    piece_rows = width // 2
    shapes = [grad_up.shape, grad_down.shape] + [(width, width)] * 4
    pieces = [r * c // (2 * piece_rows * width) for r, c in shapes]
    total = sum(pieces)
    halo_pair = halo_got.shape[1] // nodes
    vmem = pl.BlockSpec(memory_space=pltpu.VMEM)
    anywhere = pl.BlockSpec(memory_space=pl.ANY)
    dma = pltpu.SemaphoreType.DMA
    return pl.pallas_call(
        functools.partial(backward_kernel, head_dim, q_block, key_chunk, rows, pieces),
        out_shape=[jax.ShapeDtypeStruct((rows, width), BF16)] + [jax.ShapeDtypeStruct(shape, F32) for shape in shapes] + [jax.ShapeDtypeStruct((width, 2 * head_dim), F32)],
        in_specs=[vmem] * 18 + [anywhere] * 2,
        out_specs=[vmem] + [anywhere] * 7,
        scratch_shapes=[
            pltpu.VMEM((2, 2 * head_dim, q_block), BF16),
            pltpu.VMEM((2, 2 * head_dim, q_block), BF16),
            pltpu.VMEM((units, 1, q_block), F32),
            pltpu.VMEM((units, 1, q_block), F32),
            pltpu.VMEM((2, key_chunk, q_block), BF16),
            pltpu.VMEM((2, key_chunk, q_block), BF16),
            pltpu.VMEM((units, head_dim, q_block), F32),
            pltpu.VMEM((width, rows), BF16),
            pltpu.VMEM((4, rows, 2 * head_dim), F32),
            pltpu.VMEM((3, rows, 2 * head_dim), F32),
            pltpu.VMEM((rows, 2 * head_dim), F32),
            pltpu.VMEM((4, width, width), F32),
            pltpu.VMEM((total, piece_rows, width), F32),
            pltpu.VMEM((total, piece_rows, width), F32),
            pltpu.VMEM((total, piece_rows, width), F32),
            pltpu.VMEM((width, 2 * head_dim), F32),
            pltpu.VMEM((2, piece_rows, 2 * head_dim), F32),
            pltpu.VMEM((2, piece_rows, 2 * head_dim), F32),
            pltpu.VMEM((nodes, halo_pair, width), BF16),
            pltpu.VMEM((nodes, halo_pair, width), BF16),
            pltpu.VMEM((rows, width), F32),
            dma((2, total)), dma((3, total)), dma((3, total)), dma((3,)), dma((3,)), dma, dma((3,)), dma((3,)), dma((nodes,)), dma((nodes,)),
        ],
        compiler_params=pltpu.CompilerParams(vmem_limit_bytes=62 << 20, collective_id=1, has_side_effects=True),
        cost_estimate=pl.CostEstimate(flops=10 * heads * rows * keys * head_dim, bytes_accessed=40 << 20, transcendentals=heads * rows * keys),
        name='backward',
    )(counts, q_t, do_t, o_t, lse, kv, kv_t, hidden_in, x_feat, agg_msg, d_z, d_pre, adjacency_t, halo_got, w_msg, w_self, w_q_t, w_kv, grad_up, grad_down)


def solution(mesh):
    nodes = mesh.shape['nodes']
    row_spec = P(('graphs', 'nodes'), None)
    flat_spec = P(('graphs', 'nodes'))
    halo_spec = P(('graphs', 'nodes'), None, None)
    grad_spec = P('graphs', None)

    def device_step(x_feat, valid, halo_slot, edge_src, edge_dst, edge_mask, bal_perm, pos_enc, y_cot, w_msg, w_self, w_q, w_k, w_v, w_o, w_up, w_down):
        rows_dev, width = x_feat.shape
        head_dim = w_k.shape[1]
        me = lax.axis_index('nodes')
        halo_pair = halo_slot.shape[2]

        lane_owner = jnp.arange(rows_dev)[None, :] // halo_pair
        wanted = jnp.where(lane_owner == me, jnp.tile(halo_slot.reshape(nodes, halo_pair), (1, rows_dev // halo_pair)), -1)
        meta = jnp.concatenate([bal_perm[None, :], valid[None, :], wanted, jnp.zeros((6 - nodes, rows_dev), jnp.int32)], axis=0)
        w_kv = jnp.concatenate([w_k, w_v], axis=1)
        w_q_t = w_q.T
        q_t, kv_all, kv_all_t, hidden_in, agg_msg, pre_act, adjacency_t, slots, counts = front(meta, x_feat, pos_enc, edge_src, edge_dst, edge_mask, w_q_t, w_kv, w_msg, w_self, nodes, halo_pair)
        mixed_t, lse = attention_forward(counts, q_t, kv_all, kv_all_t, head_dim, rows_dev)
        u_part = dot(mixed_t, w_o, TN).astype(BF16).astype(F32)
        x_wide = x_feat.astype(F32)
        z_mid = (x_wide + jax.nn.relu(pre_act) + x_wide + u_part).astype(BF16)
        h_pre = dot(z_mid, w_up)
        hidden, gelu_pull = jax.vjp(jax.nn.gelu, h_pre)
        hidden = hidden.astype(BF16)
        keep_row = valid[:, None] > 0
        y_out = jnp.where(keep_row, z_mid.astype(F32) + dot(hidden, w_down), 0.0).astype(BF16)

        g_out = jnp.where(keep_row, y_cot, jnp.zeros_like(y_cot))
        grad_down = dot(hidden, g_out, TN)
        d_hidden = dot(g_out, w_down, NT).astype(BF16)
        d_hpre = gelu_pull(d_hidden.astype(F32))[0].astype(BF16)
        grad_up = dot(z_mid, d_hpre, TN)
        d_z = (g_out.astype(F32) + dot(d_hpre, w_up, NT)).astype(BF16)
        d_pre = jnp.where(pre_act > 0, d_z, jnp.zeros_like(d_z))
        do_t = dot(w_o, d_z, NT).astype(BF16)
        dx_feat, grad_up, grad_down, grad_self, grad_msg, grad_o, grad_q, grad_kv = backward(counts, q_t, do_t, mixed_t, lse, kv_all, kv_all_t, hidden_in, x_feat, agg_msg, d_z, d_pre, adjacency_t, slots, w_msg, w_self, w_q_t, w_kv, grad_up, grad_down)
        grad_k, grad_v = grad_kv[:, :head_dim], grad_kv[:, head_dim:]
        return (y_out, dx_feat, grad_msg, grad_self, grad_q, grad_k, grad_v, grad_o, grad_up, grad_down)

    return jax.shard_map(device_step, mesh=mesh, in_specs=(row_spec, flat_spec, halo_spec, row_spec, row_spec, row_spec, flat_spec, row_spec, row_spec) + (P(),) * 8, out_specs=(row_spec, row_spec) + (grad_spec,) * 8, check_vma=False)
```

profile of v0, /device:TPU:0, one launch (start us, length us, event | category | flops | bytes accessed | tf_op | source)
XLA Modules:
  0.0 332.8 jit_solution(17787363838591374858)
XLA Ops:
  0.6 0.0 copy-start
  0.7 0.1 pad.5.clone
  0.8 0.7 broadcast_compare_fusion
  1.5 0.7 tile.11
  2.2 0.1 tile.12
  2.3 0.8 add_add_fusion.1.meta_ref
  3.1 1.0 copy.28
  4.0 1.0 copy.29
  5.0 0.1 pad_maximum_fusion.w_kv_ref
  5.1 0.0 copy-start.2
  5.1 1.3 copy.27
  6.4 0.0 copy-start.1
  6.5 0.0 copy-start.3
  6.5 1.2 copy-done.3
  7.7 1.0 copy-done.4
  8.7 0.8 copy-done.5
  9.6 0.8 copy-done.6
  10.4 0.8 copy-done.7
  11.2 54.6 %front.1 = (bf16[512,1024]{1,0:T(8,128)(2,1)}, bf16[4096,128]{1,0:T(8,128)(2,1)}, bf16[128,4096]{1,0:T(8,128)(2,1)}, bf16[1024,512]{1,0:T(8,128)(2,1)}, bf16[102...) custom-call(s32[8,1024]{1,0:T(8,128)S(1)} %add_add_fusion.1.meta_ref, ...), custom_call_target="tpu_custom_call" | custom-call | flops 25769803776 | bytes 20971520 | tf_op jit(solution)/shard_map/front/pallas_call | solution.py:212
  65.8 0.0 copy-done.2
  65.8 0.0 copy-done.1
  65.8 0.0 copy-start.13
  65.8 0.0 copy-start.14
  65.8 0.0 copy-start.9
  65.8 1.2 copy-done.9
  67.0 1.2 copy-done.10
  68.2 1.2 copy-done.11
  69.5 52.0 %attention_fwd.1 = (bf16[512,1024]{1,0:T(8,128)(2,1)S(1)}, f32[8,1024]{1,0:T(8,128)S(1)}) custom-call(s32[4,512]{1,0:T(4,128)S(1)} %get-tuple-element.30.count_ref, bf16[512,1024]{1,0:T(8,128)(2,1)S(1)} %copy-done.9, bf16[4096,128]{1,0:T(8,128)(2,1)S(1)} %copy-done.10, bf16[128,4096]{1,0:T(8,128)(2,1)S(1)} %copy-done.11), custom_call_target="tpu_custom_call" | custom-call | flops 8589934592 | bytes 4194304 | tf_op jit(solution)/shard_map/attention_fwd/pallas_call | solution.py:298
  121.5 0.0 copy-done.13
  121.5 0.0 copy-done.14
  121.5 0.0 copy-start.8
  121.5 0.0 copy-start.12
  121.5 0.0 copy-done
  121.5 0.0 copy-done.22
  121.5 0.0 copy-done.23
  121.5 0.0 copy-start.19
  121.6 0.8 fusion.11
  122.3 0.0 copy-done.20
  122.4 2.3 fusion.19
  124.7 0.0 copy-done.8
  124.7 0.0 copy-done.12
  124.7 0.0 copy-done.19
  124.7 0.0 copy-start.21
  124.7 4.1 %select_convert_fusion = bf16[1024,512]{1,0:T(8,128)(2,1)} fusion(bf16[1024,512]{1,0:T(8,128)(2,1)S(1)} %fusion.11, bf16[2048,512]{1,0:T(8,128)(2,1)S(1)} %copy-done.19, pred[1024]{0:T(1024)(128)(4,1)S(1)} %broadcast_compare_fusion, f32[1024,2048]{1,0:T(8,128)S(1)} %fusion.19), kind=kOutput, calls=%fused_computation.19 | convolution fusion | flops 2168455168 | bytes 12583936 | tf_op jit(solution)/shard_map/dot_general | solution.py:23
  128.9 0.0 copy-done.21
  128.9 7.3 %fusion.2 = bf16[1024,2048]{1,0:T(8,128)(2,1)S(1)} fusion(f32[1024,2048]{1,0:T(8,128)S(1)} %fusion.19, bf16[2048,512]{1,0:T(8,128)(2,1)S(1)} %copy-done.19, bf16[1024,512]{1,0:T(8,128)(2,1)S(1)} %copy-done.21, pred[1024]{0:T(1024)(128)(4,1)S(1)} %broadcast_compare_fusion), kind=kOutput, calls=%fused_computation.6 | convolution fusion | flops 2194145280 | bytes 15729664 | tf_op jit(solution)/shard_map/dot_general | solution.py:23
  136.2 5.8 %fusion.17.down_ref = f32[2048,512]{1,0:T(8,128)} fusion(bf16[1024,512]{1,0:T(8,128)(2,1)S(1)} %copy-done.21, pred[1024]{0:T(1024)(128)(4,1)S(1)} %broadcast_compare_fusion, f32[1024,2048]{1,0:T(8,128)S(1)} %fusion.19), kind=kOutput, calls=%fused_computation.37 | convolution fusion | flops 2166882304 | bytes 13632512 | tf_op jit(solution)/shard_map/dot_general | solution.py:23
  142.0 3.5 %compare_select_fusion = (bf16[1024,512]{1,0:T(8,128)(2,1)}, bf16[1024,512]{1,0:T(8,128)(2,1)S(1)}) fusion(f32[1024,512]{1,0:T(8,128)S(1)} %copy-done.23, bf16[1024,2048]{1,0:T(8,128)(2,1)S(1)} %fusion.2, bf16[512,2048]{1,0:T(8,128)(2,1)S(1)} %copy-done.20, bf16[1024,512]{1,0:T(8,128)(2,1)S(1)} %copy-done.21, pred[1024]{0:T(1024)(128)(4,1)S(1)} %broadcast_compare_fusion), kind=kOutput, calls=%fused_computation.20 | convolution fusion | flops 2150629376 | bytes 11535360 | tf_op jit(solution)/shard_map/dot_general | solution.py:23
  145.5 4.4 %fusion.20.up_ref = f32[512,2048]{1,0:T(8,128)} fusion(bf16[1024,512]{1,0:T(8,128)(2,1)S(1)} %fusion.11, bf16[1024,2048]{1,0:T(8,128)(2,1)S(1)} %fusion.2), kind=kOutput, calls=%fused_computation.40 | convolution fusion | flops 2147483648 | bytes 9437184 | tf_op jit(solution)/shard_map/dot_general | solution.py:23
  149.9 1.7 fusion.12.do_ref
  151.6 0.0 copy-done.24
  151.6 165.2 %backward.1 = (bf16[1024,512]{1,0:T(8,128)(2,1)}, f32[512,2048]{1,0:T(8,128)}, f32[2048,512]{1,0:T(8,128)}, f32[512,512]{1,0:T(8,128)}, f32[512,512]{1,0:T(8,128...) custom-call(s32[4,512]{1,0:T(4,128)} %copy-done.13, bf16[512,1024]{1,0:T(8,128)(2,1)} %get-tuple-element.31.q_ref, ...), custom_call_target="tpu_custom_call" | custom-call | flops 21474836480 | bytes 41943040 | tf_op jit(solution)/shard_map/backward/pallas_call | solution.py:592
  316.9 0.0 copy-start.18
  316.9 1.3 fusion.18
  318.2 0.8 copy.32
  319.0 0.8 copy.31
  319.8 2.4 copy.41
  322.2 2.4 copy.42
  324.6 2.3 copy.43
  326.9 1.0 copy.44
  327.8 1.0 copy.45
  328.8 2.0 copy.46
  330.8 0.0 copy-done.15
  330.8 2.0 copy.47
  (19 shorter events, 0.0 us)
Async XLA Ops:
  0.6 120.9 %copy-start = (bf16[512,512]{1,0:T(8,128)(2,1)S(1)}, bf16[512,512]{1,0:T(8,128)(2,1)}, u32[]{:S(2)}) copy-start(bf16[512,512]{1,0:T(8,128)(2,1)} %param.31) | copy-start | bytes 1572868
  5.1 60.6 %copy-start.2 = (bf16[512,128]{1,0:T(8,128)(2,1)}, bf16[512,128]{1,0:T(8,128)(2,1)S(1)}, u32[]{:S(2)}) copy-start(bf16[512,128]{1,0:T(8,128)(2,1)S(1)} %pad_maximum_fusion.w_kv_ref) | copy-start | bytes 393220
  6.4 59.3 %copy-start.1 = (bf16[512,512]{0,1:T(8,128)(2,1)}, bf16[512,512]{0,1:T(8,128)(2,1)S(1)}, u32[]{:S(2)}) copy-start(bf16[512,512]{0,1:T(8,128)(2,1)S(1)} %copy.27) | copy-start | bytes 1572868
  6.5 1.2 copy-start.3
  7.7 1.0 copy-start.4
  8.7 0.8 copy-start.5
  9.6 0.8 copy-start.6
  10.4 0.8 copy-start.7
  65.8 55.7 %copy-start.13 = (s32[4,512]{1,0:T(4,128)}, s32[4,512]{1,0:T(4,128)S(1)}, u32[]{:S(2)}) copy-start(s32[4,512]{1,0:T(4,128)S(1)} %get-tuple-element.30.count_ref) | copy-start | bytes 24580
  65.8 55.7 %copy-start.14 = (s32[1,128]{1,0:T(1,128)}, s32[1,128]{1,0:T(1,128)S(1)}, u32[]{:S(2)}) copy-start(s32[1,128]{1,0:T(1,128)S(1)} %get-tuple-element.39.slot_ref) | copy-start | bytes 1540
  65.8 1.2 copy-start.9
  67.0 1.2 copy-start.10
  68.2 1.2 copy-start.11
  69.5 52.1 %copy-start.22 = (bf16[1024,512]{1,0:T(8,128)(2,1)S(1)}, bf16[1024,512]{1,0:T(8,128)(2,1)}, u32[]{:S(2)}) copy-start(bf16[1024,512]{1,0:T(8,128)(2,1)} %x_ref.3) | copy-start | bytes 3145732
  69.5 52.1 %copy-start.23 = (f32[1024,512]{1,0:T(8,128)S(1)}, f32[1024,512]{1,0:T(8,128)}, u32[]{:S(2)}) copy-start(f32[1024,512]{1,0:T(8,128)} %get-tuple-element.29) | copy-start | bytes 6291460
  69.5 52.9 %copy-start.20 = (bf16[512,2048]{1,0:T(8,128)(2,1)S(1)}, bf16[512,2048]{1,0:T(8,128)(2,1)}, u32[]{:S(2)}) copy-start(bf16[512,2048]{1,0:T(8,128)(2,1)} %param.32) | copy-start | bytes 6291460
  121.5 3.2 copy-start.8
  121.5 3.2 copy-start.12
  121.5 3.2 copy-start.19
  124.7 4.2 %copy-start.21 = (bf16[1024,512]{1,0:T(8,128)(2,1)S(1)}, bf16[1024,512]{1,0:T(8,128)(2,1)}, u32[]{:S(2)}) copy-start(bf16[1024,512]{1,0:T(8,128)(2,1)} %param.25) | copy-start | bytes 3145732
  145.5 6.1 %copy-start.24 = (bf16[1024,512]{1,0:T(8,128)(2,1)}, bf16[1024,512]{1,0:T(8,128)(2,1)S(1)}, u32[]{:S(2)}) copy-start(bf16[1024,512]{1,0:T(8,128)(2,1)S(1)} %get-tuple-element.61.dz_ref) | copy-start | bytes 3145732
  316.9 10.0 %copy-start.18 = (f32[512,512]{1,0:T(8,128)S(1)}, f32[512,512]{1,0:T(8,128)}, u32[]{:S(2)}) copy-start(f32[512,512]{1,0:T(8,128)} %get-tuple-element.76) | copy-start | bytes 3145732
  316.9 10.9 %copy-start.17 = (f32[512,512]{1,0:T(8,128)S(1)}, f32[512,512]{1,0:T(8,128)}, u32[]{:S(2)}) copy-start(f32[512,512]{1,0:T(8,128)} %get-tuple-element.79) | copy-start | bytes 3145732
  319.8 9.0 %copy-start.16 = (f32[512,2048]{1,0:T(8,128)S(1)}, f32[512,2048]{1,0:T(8,128)}, u32[]{:S(2)}) copy-start(f32[512,2048]{1,0:T(8,128)} %get-tuple-element.80) | copy-start | bytes 12582916
  322.2 8.6 %copy-start.15 = (f32[2048,512]{1,0:T(8,128)S(1)}, f32[2048,512]{1,0:T(8,128)}, u32[]{:S(2)}) copy-start(f32[2048,512]{1,0:T(8,128)} %get-tuple-element.81) | copy-start | bytes 12582916
where the time goes:
time: 334 us; the launch traced here: 333 us
  Pallas kernels  272 us (81%)
  matrix products  30 us (9%)
  local copies, waits for them, and re-layouts  28.5 us (9%)
    pallas_call x1, Pallas kernels, backward(): pl.pallas_call(functools.partial(backward_kernel, head_dim, q_block, key_...  165 us
    pallas_call x1, Pallas kernels, front(): pl.pallas_call(front_kernel, out_shape=[jax.ShapeDtypeStruct(shape, dtype...  54.6 us
    pallas_call x1, Pallas kernels, attention_forward(): pl.pallas_call(functools.partial(attention_fwd_kernel, head_dim, q_block,...  52 us
    dot_general x8, matrix products, dot(): return lax.dot_general(a, b, dims, preferred_element_type=F32)  30 us
    unnamed x62, local copies, waits for them, and re-layouts  26.3 us

commit v1 on v0

v1 whole, which is shorter than its diff:
```python
import functools
import math

import jax
import jax.numpy as jnp
from jax import lax
from jax.experimental import pallas as pl
from jax.experimental.pallas import tpu as pltpu
from jax.sharding import PartitionSpec as P

NEG_FILL = -1e30
LOG2E = math.log2(math.e)
TAIL = 32
F32 = jnp.float32
BF16 = jnp.bfloat16
NN = (((1,), (0,)), ((), ()))
NT = (((1,), (1,)), ((), ()))
TN = (((0,), (0,)), ((), ()))
TT = (((0,), (1,)), ((), ()))


def dot(a, b, dims=NN):
    return lax.dot_general(a, b, dims, preferred_element_type=F32)


def remote(src, dst, send, recv, peer):
    return pltpu.make_async_remote_copy(src_ref=src, dst_ref=dst, send_sem=send, recv_sem=recv, device_id={'nodes': peer}, device_id_type=pl.DeviceIdType.MESH)


def neighbours():
    me = lax.axis_index('nodes')
    chip, side = me // 2, lax.rem(me, 2)
    return me, chip, side, chip * 2 + 1 - side, (1 - chip) * 2 + side, (1 - chip) * 2 + 1 - side


def meet(peers):
    barrier = pltpu.get_barrier_semaphore()
    for peer in peers:
        pl.semaphore_signal(barrier, inc=1, device_id={'nodes': peer}, device_id_type=pl.DeviceIdType.MESH)
    pl.semaphore_wait(barrier, len(peers))


CHUNKS, EDGE_STEP, POS_PIECES, KV_PIECES = 4, 512, 4, 2


def front_kernel(meta_ref, x_ref, pos_ref, src_ref, dst_ref, on_ref, w_qt_ref, w_kt_ref, w_vt_ref, w_msg_ref, w_self_ref, q_ref, kv_ref, kvt_ref, hid_ref, agg_ref, pre_ref, adj_ref, slot_ref, count_ref, meta_all, pos_all, pos_acc, counts_acc, edge_acc, halo_out, halo_in, kv_all, meta_send, meta_recv, pos_send, pos_recv, halo_send, halo_recv, kv_send, kv_recv):
    rows_dev, width = x_ref.shape
    table_rows = adj_ref.shape[0]
    half = rows_dev // 2
    nodes = meta_all.shape[0]
    halo_pair = halo_in.shape[1]
    me, chip, side, mate, cross, other = neighbours()
    peers = (mate, cross, other)
    meet(peers)

    meta_copies = [remote(meta_ref, meta_all.at[me], meta_send.at[i], meta_recv.at[me], peer) for i, peer in enumerate(peers)]
    for copy in meta_copies:
        copy.start()
    piece = rows_dev // POS_PIECES

    def pos_rows(index):
        return pl.ds(index * piece, piece)

    pos_to_cross = [remote(pos_ref.at[pos_rows(k), :], pos_all.at[me, pos_rows(k), :], pos_send.at[0, k], pos_recv.at[0, k], cross) for k in range(POS_PIECES)]
    pos_to_mate = [remote(pos_ref.at[pos_rows(k), :], pos_all.at[me, pos_rows(k), :], pos_send.at[1, k], pos_recv.at[1, k], mate) for k in range(POS_PIECES)]
    pos_relay = [remote(pos_all.at[cross, pos_rows(k), :], pos_all.at[cross, pos_rows(k), :], pos_send.at[2, k], pos_recv.at[2, k], mate) for k in range(POS_PIECES)]
    for copy in pos_to_cross + pos_to_mate:
        copy.start()
    meta_all[me] = meta_ref[...]

    def relay_pos(k):
        pos_to_cross[k].wait_recv()
        pos_relay[k].start()

    def place_pos(owner, source, first):
        perm = meta_all[owner, 0:1, :] - me * rows_dev
        size = 256

        def body(index, carry):
            rows = pl.ds(pl.multiple_of(index * size, size), size)
            hot = jnp.where(index * size + lax.broadcasted_iota(jnp.int32, (size, rows_dev), 0) == perm, 1.0, 0.0).astype(BF16)
            part = dot(hot, source[...])
            pos_acc[rows, :] = part if first else pos_acc[rows, :] + part
            return carry

        lax.fori_loop(0, rows_dev // size, body, 0)

    edges = src_ref.shape[1]
    steps = edges // (CHUNKS * EDGE_STEP)
    assert CHUNKS * EDGE_STEP * steps == edges and EDGE_STEP * steps < 4096

    def edge_block(index):
        cols = pl.ds(pl.multiple_of(index * EDGE_STEP, EDGE_STEP), EDGE_STEP)
        src, dst, on = src_ref[:, cols], dst_ref[:, cols], on_ref[:, cols]
        upper = dst >= half
        place = jnp.where(upper, dst - half, dst)
        weight = jnp.where(on > 0, jnp.where(upper, 4096.0, 1.0), 0.0)
        src_hot = jnp.where(lax.broadcasted_iota(jnp.int32, (table_rows, EDGE_STEP), 0) == src, 1.0, 0.0).astype(BF16)
        dst_hot = jnp.where(lax.broadcasted_iota(jnp.int32, (half, EDGE_STEP), 0) == place, weight, 0.0).astype(BF16)
        return dot(src_hot, dst_hot, NT)

    def count_chunk(chunk):
        edge_acc[...] = jnp.zeros_like(edge_acc)

        def body(step, carry):
            edge_acc[...] += edge_block(chunk * steps + step)
            return carry

        lax.fori_loop(0, steps, body, 0)
        total = edge_acc[...]
        high = jnp.floor(total * (1.0 / 4096.0))
        low = total - high * 4096.0
        if chunk == 0:
            counts_acc[:, :half] = low
            counts_acc[:, half:] = high
        elif chunk < CHUNKS - 1:
            counts_acc[:, :half] += low
            counts_acc[:, half:] += high
        else:
            adj_ref[:, :half] = (counts_acc[:, :half] + low).astype(BF16)
            adj_ref[:, half:] = (counts_acc[:, half:] + high).astype(BF16)

    def halo_copy(peer, owner):
        return remote(halo_out.at[peer], halo_in.at[owner], halo_send.at[peer], halo_recv.at[owner], peer)

    count_chunk(0)
    for peer in peers:
        remote(meta_ref, meta_all.at[peer], meta_send.at[0], meta_recv.at[peer], peer).wait_recv()
    tables = meta_all[0, :, 0:nodes * halo_pair]
    for node in range(1, nodes):
        tables = jnp.maximum(tables, meta_all[node, :, 0:nodes * halo_pair])
    tables = jnp.where(lax.broadcasted_iota(jnp.int32, tables.shape, 0) == 2 + me, tables, -1)
    slots = jnp.max(tables.astype(F32), axis=0, keepdims=True).astype(jnp.int32)
    slot_ref[...] = slots
    slot_hot = jnp.where(lax.broadcasted_iota(jnp.int32, (rows_dev, nodes * halo_pair), 0) == slots, 1.0, 0.0).astype(BF16)
    halo_out[...] = dot(slot_hot, x_ref[...], TN).astype(BF16).reshape(halo_out.shape)
    relay_pos(0)
    place_pos(me, pos_ref, True)
    for peer in peers:
        halo_copy(peer, me).start()
    halo_in[me] = halo_out[me]
    for node in range(nodes):
        held = jnp.sum(meta_all[node, 1:2, :].astype(F32), axis=1, keepdims=True).astype(jnp.int32)
        count_ref[node:node + 1, :] = jnp.broadcast_to(held, (1, count_ref.shape[1]))
    count_chunk(1)
    relay_pos(1)
    for copy in pos_to_mate:
        copy.wait_recv()
    place_pos(mate, pos_all.at[mate], False)
    count_chunk(2)
    relay_pos(2)
    count_chunk(3)
    relay_pos(3)
    place_pos(cross, pos_all.at[cross], False)
    for copy in pos_relay:
        copy.wait_recv()
    place_pos(other, pos_all.at[other], False)

    hid_ref[...] = (x_ref[...].astype(F32) + pos_acc[...]).astype(BF16)
    kv_all[me] = dot(hid_ref[...], jnp.concatenate([w_kt_ref[...], w_vt_ref[...]], axis=0), NT).astype(BF16)
    q_ref[...] = dot(w_qt_ref[...], hid_ref[...], NT).astype(BF16)
    kv_piece = rows_dev // KV_PIECES

    def kv_copy(owner, k, kind, peer):
        rows = pl.ds(k * kv_piece, kv_piece)
        return remote(kv_all.at[owner, rows, :], kv_all.at[owner, rows, :], kv_send.at[kind, k], kv_recv.at[kind, k], peer)

    kv_to_cross = [kv_copy(me, k, 0, cross) for k in range(KV_PIECES)]
    kv_to_mate = [kv_copy(me, k, 1, mate) for k in range(KV_PIECES)]
    kv_relay = [kv_copy(cross, k, 2, mate) for k in range(KV_PIECES)]
    for copy in kv_to_cross + kv_to_mate:
        copy.start()
    size = kv_all.shape[2]
    eye = jnp.where(lax.broadcasted_iota(jnp.int32, (size, size), 0) == lax.broadcasted_iota(jnp.int32, (size, size), 1), 1.0, 0.0).astype(BF16)

    def keep_kv(owner):
        rows = pl.ds(pl.multiple_of(owner * rows_dev, rows_dev), rows_dev)
        kv_ref[rows, :] = kv_all[owner]
        kvt_ref[:, rows] = dot(eye, kv_all[owner], NT).astype(BF16)

    for peer in peers:
        halo_copy(me, peer).wait_recv()
    agg = dot(adj_ref[:rows_dev, :], x_ref[...], TN) + dot(adj_ref[rows_dev:, :], halo_in[...].reshape(nodes * halo_pair, width), TN)
    agg_ref[...] = agg.astype(BF16)
    keep_kv(me)
    kv_to_cross[0].wait_recv()
    kv_relay[0].start()
    pre_ref[...] = dot(agg_ref[...], w_msg_ref[...]) + dot(x_ref[...], w_self_ref[...])
    for k in range(1, KV_PIECES):
        kv_to_cross[k].wait_recv()
        kv_relay[k].start()
    for copy in kv_to_mate:
        copy.wait_recv()
    keep_kv(mate)
    keep_kv(cross)
    for copy in kv_relay:
        copy.wait_recv()
    keep_kv(other)
    for copy in meta_copies + pos_to_cross + pos_to_mate + pos_relay + [halo_copy(peer, me) for peer in peers] + kv_to_cross + kv_to_mate + kv_relay:
        copy.wait_send()


def front(meta, x_feat, pos_enc, edge_src, edge_dst, edge_mask, w_q_t, w_k_t, w_v_t, w_msg, w_self, nodes, halo_pair):
    rows, width = x_feat.shape
    pair = 2 * w_k_t.shape[0]
    keys = nodes * rows
    table_rows = rows + nodes * halo_pair
    vmem = pl.BlockSpec(memory_space=pltpu.VMEM)
    dma = pltpu.SemaphoreType.DMA
    out = [((width, rows), BF16), ((keys, pair), BF16), ((pair, keys), BF16), ((rows, width), BF16), ((rows, width), BF16), ((rows, width), F32), ((table_rows, rows), BF16), ((1, nodes * halo_pair), jnp.int32), ((nodes, 512), jnp.int32)]
    return pl.pallas_call(
        front_kernel,
        out_shape=[jax.ShapeDtypeStruct(shape, dtype) for shape, dtype in out],
        in_specs=[vmem] * 11,
        out_specs=[vmem] * len(out),
        scratch_shapes=[
            pltpu.VMEM((nodes,) + meta.shape, jnp.int32),
            pltpu.VMEM((nodes, rows, width), BF16),
            pltpu.VMEM((rows, width), F32),
            pltpu.VMEM((table_rows, rows), F32),
            pltpu.VMEM((table_rows, rows // 2), F32),
            pltpu.VMEM((nodes, halo_pair, width), BF16),
            pltpu.VMEM((nodes, halo_pair, width), BF16),
            pltpu.VMEM((nodes, rows, pair), BF16),
            dma((3,)), dma((nodes,)), dma((3, POS_PIECES)), dma((3, POS_PIECES)), dma((nodes,)), dma((nodes,)), dma((3, KV_PIECES)), dma((3, KV_PIECES)),
        ],
        compiler_params=pltpu.CompilerParams(vmem_limit_bytes=52 << 20, collective_id=2, has_side_effects=True),
        cost_estimate=pl.CostEstimate(flops=24 << 30, bytes_accessed=20 << 20, transcendentals=0),
        name='front',
    )(meta, x_feat, pos_enc, edge_src, edge_dst, edge_mask, w_q_t, w_k_t, w_v_t, w_msg, w_self)


def mask_tail(scores, chunk, key_chunk, part_rows, count_ref):
    start = chunk * key_chunk
    part = start // part_rows
    first = start - part * part_rows + key_chunk - TAIL
    row_ix = first + lax.broadcasted_iota(jnp.int32, (TAIL, scores.shape[1]), 0)
    tail = jnp.where(row_ix < count_ref[pl.ds(part, 1), :scores.shape[1]], scores[key_chunk - TAIL:, :], NEG_FILL)
    return jnp.concatenate([scores[:key_chunk - TAIL, :], tail], axis=0)


def attention_fwd_kernel(head_dim, q_block, key_chunk, part_rows, count_ref, q_ref, kv_ref, kvt_ref, out_ref, lse_ref, w_q, s_buf, stat):
    heads = q_ref.shape[0] // head_dim
    blocks = q_ref.shape[1] // q_block
    units = heads * blocks
    keys = kv_ref.shape[0]
    chunks = keys // key_chunk
    factor = head_dim ** -0.5 * LOG2E
    groups = key_chunk // 8

    def load_weights(unit):
        head, block = unit // blocks, lax.rem(unit, blocks)
        w_q[:head_dim, :] = q_ref[pl.ds(pl.multiple_of(head * head_dim, head_dim), head_dim), pl.ds(pl.multiple_of(block * q_block, q_block), q_block)]

    def score_stage(slot, chunk, run_max):
        rows = pl.ds(pl.multiple_of(chunk * key_chunk, key_chunk), key_chunk)
        scores = mask_tail(dot(kv_ref[rows, :], w_q[...]), chunk, key_chunk, part_rows, count_ref)
        s_buf[slot, rows, :] = scores
        return jnp.maximum(run_max, jnp.max(scores.reshape(groups, 8, q_block), axis=0))

    w_q[head_dim:, :] = jnp.zeros((w_q.shape[0] - head_dim, q_block), BF16)
    floor = jnp.full((8, q_block), -jnp.inf, F32)
    load_weights(0)
    stat[...] = lax.fori_loop(0, chunks, lambda chunk, run_max: score_stage(0, chunk, run_max), floor)

    def unit_body(unit, carry):
        slot = lax.rem(unit, 2)
        load_weights(jnp.minimum(unit + 1, units - 1))
        top = jnp.max(stat[...], axis=0, keepdims=True) * factor

        def chunk_body(chunk, state):
            run_max, run_sum, weighted = state
            cols = pl.ds(pl.multiple_of(chunk * key_chunk, key_chunk), key_chunk)
            prob = jnp.exp2(s_buf[slot, cols, :] * factor - top)
            run_sum = run_sum + jnp.sum(prob.reshape(groups, 8, q_block), axis=0)
            weighted = weighted + dot(kvt_ref[head_dim:2 * head_dim, cols], prob.astype(BF16))
            return score_stage(1 - slot, chunk, run_max), run_sum, weighted

        run_max, run_sum, weighted = lax.fori_loop(0, chunks, chunk_body, (floor, jnp.zeros((8, q_block), F32), jnp.zeros((head_dim, q_block), F32)))
        stat[...] = run_max
        total = jnp.sum(run_sum, axis=0, keepdims=True)
        head, block = unit // blocks, lax.rem(unit, blocks)
        cols = pl.ds(pl.multiple_of(block * q_block, q_block), q_block)
        out_ref[pl.ds(pl.multiple_of(head * head_dim, head_dim), head_dim), cols] = (weighted / total).astype(BF16)
        lse_ref[pl.ds(head, 1), cols] = top + jnp.log2(total)
        return carry

    lax.fori_loop(0, units, unit_body, 0)


def attention_forward(counts, q_t, kv, kv_t, head_dim, part_rows):
    width, rows = q_t.shape
    keys = kv.shape[0]
    heads = width // head_dim
    q_block, key_chunk = 256, 1024
    vmem = pl.BlockSpec(memory_space=pltpu.VMEM)
    return pl.pallas_call(
        functools.partial(attention_fwd_kernel, head_dim, q_block, key_chunk, part_rows),
        out_shape=[jax.ShapeDtypeStruct((width, rows), BF16), jax.ShapeDtypeStruct((heads, rows), F32)],
        in_specs=[vmem] * 4,
        out_specs=[vmem, vmem],
        scratch_shapes=[pltpu.VMEM((2 * head_dim, q_block), BF16), pltpu.VMEM((2, keys, q_block), F32), pltpu.VMEM((8, q_block), F32)],
        compiler_params=pltpu.CompilerParams(vmem_limit_bytes=48 << 20),
        cost_estimate=pl.CostEstimate(flops=4 * heads * rows * keys * head_dim, bytes_accessed=4 << 20, transcendentals=heads * rows * keys),
        name='attention_fwd',
    )(counts, q_t, kv, kv_t)


FINAL_STEPS, FINAL_LAG = 14, 1
HOLD_STEP = 68
ROW_BLOCK = 256
GELU_A, GELU_B = math.sqrt(2.0 / math.pi), 0.044715


def backward_kernel(head_dim, q_block, key_chunk, part_rows, count_ref, q_ref, o_ref, lse_ref, kv_ref, kvt_ref, hid_ref, x_ref, agg_ref, adj_ref, slot_ref, w_msg_ref, w_self_ref, w_qt_ref, w_kt_ref, w_vt_ref, w_o_ref, pre_hbm, cot_hbm, up_hbm, down_hbm, *rest):
    y_ref, dx_ref, rest = rest[0], rest[1], rest[2:]
    sum_refs, kv_sum_ref, rest = rest[:6], rest[6], rest[7:]
    do_buf, dz_buf, dpre_buf, dx_acc, dkv_in, dkv_sum, local, from_mate, from_cross, kv_local, kv_own, kv_in, halo_out, halo_in, load_sem, keep_sem, send_sem, recv_sem, dkv_send, dkv_recv, kv_sem, kv_send, kv_recv, halo_send, halo_recv = rest
    heads = q_ref.shape[0] // head_dim
    blocks = q_ref.shape[1] // q_block
    units = heads * blocks
    chunks = kv_ref.shape[0] // key_chunk
    steps = units * chunks
    per_group = steps // 4
    halves = part_rows // key_chunk
    scale = head_dim ** -0.5
    factor = scale * LOG2E
    total, width = local.shape[0], local.shape[1]
    half_rows = width // 2
    ffn_chunks = up_hbm.shape[1] // width
    first_small = 2 * ffn_chunks
    me, chip, side, mate, cross, other = neighbours()

    def block(index, half):
        if index >= first_small:
            return sum_refs[2 + index - first_small].at[pl.ds(half * half_rows, half_rows), :]
        chunk = index // 2
        if index % 2 == 0:
            return sum_refs[1].at[pl.ds(chunk * width + half * half_rows, half_rows), :]
        return sum_refs[0].at[pl.ds(half * half_rows, half_rows), pl.ds(chunk * width, width)]

    def part(index, half):
        return local.at[index, pl.ds(half * half_rows, half_rows), :]

    def to_peer(src, dst, kind, index, peer):
        return remote(src, dst, send_sem.at[kind, index], recv_sem.at[kind, index], peer)

    def mate_copy(index):
        return to_peer(part(index, 1 - side), from_mate.at[index], 0, index, mate)

    def cross_copy(index):
        return to_peer(part(index, side), from_cross.at[index], 1, index, cross)

    def back_copy(index, half):
        return to_peer(from_mate.at[index], block(index, half), 2, index, mate)

    def keep_copy(index):
        return pltpu.make_async_copy(from_mate.at[index], block(index, side), keep_sem.at[index])

    my_half = pl.ds(pl.multiple_of(side * half_rows, half_rows), half_rows)

    def chip_sum(index):
        mate_copy(index).wait_recv()
        local[index, my_half, :] = local[index, my_half, :] + from_mate[index]

    def group_sum(index):
        cross_copy(index).wait_recv()
        from_mate[index] = local[index, my_half, :] + from_cross[index]

    def start_out(index):
        keep_copy(index).start()
        back_copy(index, side).start()

    kv_half = kv_local.shape[0] // 2

    def kv_rows(half):
        return pl.ds(half * kv_half, kv_half)

    kv_to_mate = remote(kv_local.at[kv_rows(1 - side), :], kv_in.at[0], kv_send.at[0], kv_recv.at[0], mate)
    kv_to_cross = remote(kv_own.at[0], kv_in.at[1], kv_send.at[1], kv_recv.at[1], cross)
    kv_keep = pltpu.make_async_copy(kv_own.at[1], kv_sum_ref.at[kv_rows(side), :], kv_sem)

    def kv_back(half):
        return remote(kv_own.at[1], kv_sum_ref.at[kv_rows(half), :], kv_send.at[2], kv_recv.at[2], mate)

    halo_pair = halo_out.shape[1]

    def halo_copy(peer, owner):
        return remote(halo_out.at[peer], halo_in.at[owner], halo_send.at[peer], halo_recv.at[owner], peer)

    def ffn_phase(w_up, w_down, g_buf, z_buf, y_acc, act, d_act):
        loads = [pltpu.make_async_copy(src, dst, load_sem.at[i]) for i, (src, dst) in enumerate(((pre_hbm, dx_acc), (cot_hbm, g_buf), (up_hbm, w_up), (down_hbm, w_down)))]
        for copy in loads:
            copy.start()
        meet((mate, cross, other))
        y_acc[...] = dot(o_ref[...], w_o_ref[...], TN)
        loads[0].wait()
        pre = dx_acc[...]
        x_wide = x_ref[...].astype(F32)
        z_mid = (x_wide + jnp.maximum(pre, 0.0) + x_wide + y_acc[...].astype(BF16).astype(F32)).astype(BF16)
        dpre_buf[...] = jnp.where(pre > 0, 1.0, 0.0).astype(BF16)
        z_buf[...] = z_mid
        loads[1].wait()
        keep = lax.broadcasted_iota(jnp.int32, (part_rows, width), 0) < count_ref[pl.ds(me, 1), :width]
        g_wide = jnp.where(keep, g_buf[...].astype(F32), 0.0)
        g_buf[...] = g_wide.astype(BF16)
        dx_acc[...] = g_wide
        y_acc[...] = z_mid.astype(F32)
        loads[2].wait()
        loads[3].wait()

        def ffn_chunk(chunk, carry):
            cols = pl.ds(pl.multiple_of(chunk * width, width), width)

            def row_block(index, inner):
                rows = pl.ds(pl.multiple_of(index * ROW_BLOCK, ROW_BLOCK), ROW_BLOCK)
                h_pre = dot(z_buf[rows, :], w_up[:, cols])
                square = h_pre * h_pre
                bend = jnp.tanh(h_pre * (GELU_A + GELU_A * GELU_B * square))
                gate = 0.5 + 0.5 * bend
                act[rows, :] = (h_pre * gate).astype(BF16)
                slope = gate + (0.5 * h_pre) * (1.0 - bend * bend) * (GELU_A + 3.0 * GELU_A * GELU_B * square)
                d_hidden = dot(g_buf[rows, :], w_down[cols, :], NT).astype(BF16)
                d_act[rows, :] = (d_hidden.astype(F32) * slope).astype(BF16)
                y_acc[rows, :] += dot(act[rows, :], w_down[cols, :])
                dx_acc[rows, :] += dot(d_act[rows, :], w_up[:, cols], NT)
                return inner

            lax.fori_loop(0, part_rows // ROW_BLOCK, row_block, 0)
            local[2 * chunk] = dot(act[...], g_buf[...], TN)

            @pl.when(chunk > 0)
            def sum_previous():
                chip_sum(2 * chunk - 1)

            local[2 * chunk + 1] = dot(z_buf[...], d_act[...], TN)
            mate_copy(2 * chunk).start()

            @pl.when(chunk > 0)
            def send_previous():
                cross_copy(2 * chunk - 1).start()

            chip_sum(2 * chunk)
            mate_copy(2 * chunk + 1).start()
            cross_copy(2 * chunk).start()
            return carry

        lax.fori_loop(0, ffn_chunks, ffn_chunk, 0)
        y_ref[...] = jnp.where(keep, y_acc[...], 0.0).astype(BF16)

    pl.run_scoped(ffn_phase, pltpu.VMEM(up_hbm.shape, BF16), pltpu.VMEM(down_hbm.shape, BF16), pltpu.VMEM(x_ref.shape, BF16), pltpu.VMEM(x_ref.shape, BF16), pltpu.VMEM(x_ref.shape, F32), pltpu.VMEM(x_ref.shape, BF16), pltpu.VMEM(x_ref.shape, BF16))
    d_z = dx_acc[...].astype(BF16)
    dz_buf[...] = d_z
    dpre_buf[...] = jnp.where(dpre_buf[...] > 0, d_z, jnp.zeros_like(d_z))
    chip_sum(first_small - 1)
    do_buf[...] = dot(w_o_ref[...], dz_buf[...], NT).astype(BF16)
    cross_copy(first_small - 1).start()

    d_agg = dot(dpre_buf[...], w_msg_ref[...], NT).astype(BF16)
    halo_out[...] = dot(adj_ref[part_rows:, :], d_agg).astype(BF16).reshape(halo_out.shape)
    dx_acc[...] = 2.0 * dz_buf[...].astype(F32) + dot(dpre_buf[...], w_self_ref[...], NT)
    dx_acc[...] += dot(adj_ref[:part_rows, :], d_agg)
    for peer in (mate, cross, other):
        halo_copy(peer, me).start()
    halo_in[me] = halo_out[me]
    local[first_small] = dot(x_ref[...], dpre_buf[...], TN)
    local[first_small + 1] = dot(agg_ref[...], dpre_buf[...], TN)
    local[first_small + 2] = dot(o_ref[...], dz_buf[...])

    def attention_phase(w_q, w_do, lse_buf, delta_buf, p_buf, ds_buf, dq_acc, dq_all, dkv_acc):
        dkv_copies = [remote(src, dkv_in.at[i], dkv_send.at[i], dkv_recv.at[i], peer) for i, (src, peer) in enumerate(((dkv_acc.at[0], mate), (dkv_sum, cross), (dkv_acc.at[2], mate)))]

        def unit_spots(unit):
            head, place = unit // blocks, lax.rem(unit, blocks)
            return head, pl.ds(pl.multiple_of(head * head_dim, head_dim), head_dim), pl.ds(pl.multiple_of(place * q_block, q_block), q_block)

        def prepare(unit, carry):
            head, rows, cols = unit_spots(unit)
            delta_buf[unit] = jnp.sum(do_buf[rows, cols].astype(F32) * o_ref[rows, cols].astype(F32), axis=0, keepdims=True)
            lse_buf[unit] = lse_ref[pl.ds(head, 1), cols]
            dq_acc[unit] = jnp.zeros((head_dim, q_block), F32)
            return carry

        lax.fori_loop(0, units, prepare, 0)
        for slot in range(2):
            w_q[slot, head_dim:, :] = jnp.zeros((head_dim, q_block), BF16)
            w_do[slot, :head_dim, :] = jnp.zeros((head_dim, q_block), BF16)
        dkv_acc[...] = jnp.zeros_like(dkv_acc)

        def place_of(step):
            group = step // per_group
            chunk = step // units
            owner = lax.rem(chip + 1 - group // 2, 2) * 2 + lax.rem(side + 1 - lax.rem(group, 2), 2)
            offset = lax.rem(chunk, halves) * key_chunk
            rows = pl.ds(pl.multiple_of(owner * part_rows + offset, key_chunk), key_chunk)
            return group, owner, offset, rows, lax.rem(step, units), lax.rem(step, 2)

        def first_stage(step):
            group, owner, offset, rows, unit, slot = place_of(step)
            head, unit_rows, cols = unit_spots(unit)
            w_q[slot, :head_dim, :] = q_ref[unit_rows, cols]
            w_do[slot, head_dim:, :] = do_buf[unit_rows, cols]
            kv = kv_ref[rows, :]
            scores = dot(kv, w_q[slot])
            row_ix = offset + key_chunk - TAIL + lax.broadcasted_iota(jnp.int32, (TAIL, q_block), 0)
            tail = jnp.where(row_ix < count_ref[pl.ds(owner, 1), :q_block], scores[key_chunk - TAIL:, :], NEG_FILL)
            scores = jnp.concatenate([scores[:key_chunk - TAIL, :], tail], axis=0)
            prob = jnp.exp2(scores * factor - lse_buf[unit])
            p_buf[slot] = prob.astype(BF16)
            ds_buf[slot] = (prob * (dot(kv, w_do[slot]) - delta_buf[unit])).astype(BF16)

        def second_stage(step):
            group, owner, offset, rows, unit, slot = place_of(step)
            d_scores = ds_buf[slot]
            spot = pl.ds(pl.multiple_of(offset, key_chunk), key_chunk)
            dkv_acc[group, spot, :] += dot(d_scores, w_q[slot], NT) + dot(p_buf[slot], w_do[slot], NT)
            dq_acc[unit] += dot(kvt_ref[:head_dim, rows], d_scores)

        def exchange(step):
            held = jnp.logical_and(step >= HOLD_STEP, step < HOLD_STEP + 12)
            turn = (step - HOLD_STEP) // 4 + first_small
            phase = lax.rem(step, 4)

            @pl.when(jnp.logical_and(held, phase == 1))
            def sum_chip():
                chip_sum(turn)

            @pl.when(jnp.logical_and(held, phase == 2))
            def send_cross():
                cross_copy(turn).start()

            lap, beat = step // FINAL_STEPS - FINAL_LAG, lax.rem(step, FINAL_STEPS)

            @pl.when(jnp.logical_and(lap >= 0, beat == 0))
            def sum_group():
                group_sum(lap)

            @pl.when(jnp.logical_and(lap >= 0, beat == 1))
            def send_back():
                for k in range(done):
                    @pl.when(lap == k)
                    def start_piece(k=k):
                        start_out(k)

            @pl.when(step == 3)
            def small_pieces():
                for index in range(first_small, total - 1):
                    mate_copy(index).start()

            @pl.when(step == per_group + 1)
            def first_group():
                dkv_copies[0].start()

            @pl.when(step == 2 * per_group + 1)
            def second_group():
                dkv_copies[0].wait_recv()
                dkv_sum[...] = dkv_acc[1] + dkv_in[0]

            @pl.when(step == 2 * per_group + 2)
            def send_second():
                dkv_copies[1].start()

            @pl.when(step == 3 * per_group + 1)
            def third_group():
                dkv_copies[2].start()

        done = (steps - 1) // FINAL_STEPS - FINAL_LAG + 1
        assert (steps - 1) % FINAL_STEPS >= 1 and 0 < done < total - 2 and HOLD_STEP > 2 * per_group + 2 and HOLD_STEP % 4 == 0

        first_stage(0)

        def body(step, carry):
            exchange(step)
            second_stage(step - 1)
            first_stage(step)
            return carry

        lax.fori_loop(1, steps, body, 0)
        second_stage(steps - 1)

        def gather_dq(unit, carry):
            head, rows, cols = unit_spots(unit)
            dq_all[rows, cols] = (dq_acc[unit] * scale).astype(BF16)
            return carry

        lax.fori_loop(0, units, gather_dq, 0)
        last = total - 1
        local[last] = dot(dq_all[...], hid_ref[...]).T
        dkv_copies[2].wait_recv()
        dkv_copies[1].wait_recv()
        dkv = dkv_acc[3] + dkv_in[2] + dkv_in[1]
        lane = lax.broadcasted_iota(jnp.int32, dkv.shape, 1)
        dkv = jnp.where(lane < head_dim, dkv * scale, dkv).astype(BF16)
        mate_copy(last).start()
        kv_local[...] = dot(dkv, hid_ref[...], TN)
        dx_acc[...] += dot(dkv, jnp.concatenate([w_kt_ref[...], w_vt_ref[...]], axis=0))
        kv_to_mate.start()
        chip_sum(last)
        kv_to_mate.wait_recv()
        kv_own[0] = kv_local[pl.ds(pl.multiple_of(side * kv_half, kv_half), kv_half), :] + kv_in[0]
        for peer in (mate, cross, other):
            halo_copy(me, peer).wait_recv()
        slot_hot = jnp.where(lax.broadcasted_iota(jnp.int32, (part_rows, 4 * halo_pair), 0) == slot_ref[...], 1.0, 0.0).astype(BF16)
        dx_acc[...] += dot(slot_hot, halo_in[...].reshape(4 * halo_pair, width))
        cross_copy(last).start()
        kv_to_cross.start()
        dx_ref[...] = (dx_acc[...] + dot(dq_all[...], w_qt_ref[...], TN)).astype(BF16)
        for index in range(done, total):
            group_sum(index)
            if index > done:
                start_out(index - 1)
        kv_to_cross.wait_recv()
        kv_own[1] = kv_own[0] + kv_in[1]
        start_out(last)
        kv_keep.start()
        kv_back(side).start()
        for copy in dkv_copies:
            copy.wait_send()

    pl.run_scoped(
        attention_phase,
        pltpu.VMEM((2, 2 * head_dim, q_block), BF16),
        pltpu.VMEM((2, 2 * head_dim, q_block), BF16),
        pltpu.VMEM((units, 1, q_block), F32),
        pltpu.VMEM((units, 1, q_block), F32),
        pltpu.VMEM((2, key_chunk, q_block), BF16),
        pltpu.VMEM((2, key_chunk, q_block), BF16),
        pltpu.VMEM((units, head_dim, q_block), F32),
        pltpu.VMEM((width, part_rows), BF16),
        pltpu.VMEM((4, part_rows, 2 * head_dim), F32),
    )
    for copy in [kv_to_mate, kv_to_cross, kv_back(side)] + [halo_copy(peer, me) for peer in (mate, cross, other)]:
        copy.wait_send()
    kv_keep.wait()
    kv_back(1 - side).wait_recv()
    for index in range(total):
        mate_copy(index).wait_send()
        cross_copy(index).wait_send()
        keep_copy(index).wait()
        back_copy(index, side).wait_send()
        back_copy(index, 1 - side).wait_recv()


def backward(counts, q_t, o_t, lse, kv, kv_t, hidden_in, x_feat, agg_msg, adjacency_t, slots, w_msg, w_self, w_q_t, w_k_t, w_v_t, w_o, pre_act, y_cot, w_up, w_down):
    width, rows = q_t.shape
    keys = kv.shape[0]
    head_dim = kv.shape[1] // 2
    heads = width // head_dim
    nodes = keys // rows
    q_block, key_chunk = 512, 512
    half = width // 2
    shapes = [w_up.shape, w_down.shape] + [(width, width)] * 4
    total = sum(r * c // (width * width) for r, c in shapes)
    halo_pair = slots.shape[1] // nodes
    vmem = pl.BlockSpec(memory_space=pltpu.VMEM)
    anywhere = pl.BlockSpec(memory_space=pl.ANY)
    dma = pltpu.SemaphoreType.DMA
    return pl.pallas_call(
        functools.partial(backward_kernel, head_dim, q_block, key_chunk, rows),
        out_shape=[jax.ShapeDtypeStruct((rows, width), BF16)] * 2 + [jax.ShapeDtypeStruct(shape, F32) for shape in shapes] + [jax.ShapeDtypeStruct((2 * head_dim, width), F32)],
        in_specs=[vmem] * 17 + [anywhere] * 4,
        out_specs=[vmem] * 2 + [anywhere] * 7,
        scratch_shapes=[
            pltpu.VMEM((width, rows), BF16),
            pltpu.VMEM((rows, width), BF16),
            pltpu.VMEM((rows, width), BF16),
            pltpu.VMEM((rows, width), F32),
            pltpu.VMEM((3, rows, 2 * head_dim), F32),
            pltpu.VMEM((rows, 2 * head_dim), F32),
            pltpu.VMEM((total, width, width), F32),
            pltpu.VMEM((total, half, width), F32),
            pltpu.VMEM((total, half, width), F32),
            pltpu.VMEM((2 * head_dim, width), F32),
            pltpu.VMEM((2, head_dim, width), F32),
            pltpu.VMEM((2, head_dim, width), F32),
            pltpu.VMEM((nodes, halo_pair, width), BF16),
            pltpu.VMEM((nodes, halo_pair, width), BF16),
            dma((4,)), dma((total,)), dma((3, total)), dma((3, total)), dma((3,)), dma((3,)), dma, dma((3,)), dma((3,)), dma((nodes,)), dma((nodes,)),
        ],
        compiler_params=pltpu.CompilerParams(vmem_limit_bytes=67043328, collective_id=1, has_side_effects=True),
        cost_estimate=pl.CostEstimate(flops=10 * heads * rows * keys * head_dim, bytes_accessed=40 << 20, transcendentals=heads * rows * keys),
        name='backward',
    )(counts, q_t, o_t, lse, kv, kv_t, hidden_in, x_feat, agg_msg, adjacency_t, slots, w_msg, w_self, w_q_t, w_k_t, w_v_t, w_o, pre_act, y_cot, w_up, w_down)


def solution(mesh):
    nodes = mesh.shape['nodes']
    row_spec = P(('graphs', 'nodes'), None)
    flat_spec = P(('graphs', 'nodes'))
    halo_spec = P(('graphs', 'nodes'), None, None)
    grad_spec = P('graphs', None)

    def device_step(x_feat, valid, halo_slot, edge_src, edge_dst, edge_mask, bal_perm, pos_enc, y_cot, w_msg, w_self, w_q, w_k, w_v, w_o, w_up, w_down):
        rows_dev, width = x_feat.shape
        head_dim = w_k.shape[1]
        me = lax.axis_index('nodes')
        halo_pair = halo_slot.shape[2]

        lane_owner = jnp.arange(rows_dev)[None, :] // halo_pair
        wanted = jnp.where(lane_owner == me, jnp.tile(halo_slot.reshape(nodes, halo_pair), (1, rows_dev // halo_pair)), -1)
        meta = jnp.concatenate([bal_perm[None, :], valid[None, :], wanted, jnp.zeros((6 - nodes, rows_dev), jnp.int32)], axis=0)
        w_q_t, w_k_t, w_v_t = w_q.T, w_k.T, w_v.T
        q_t, kv_all, kv_all_t, hidden_in, agg_msg, pre_act, adjacency_t, slots, counts = front(meta, x_feat, pos_enc, edge_src, edge_dst, edge_mask, w_q_t, w_k_t, w_v_t, w_msg, w_self, nodes, halo_pair)
        mixed_t, lse = attention_forward(counts, q_t, kv_all, kv_all_t, head_dim, rows_dev)
        y_out, dx_feat, grad_up, grad_down, grad_self, grad_msg, grad_o, grad_q, grad_kv = backward(counts, q_t, mixed_t, lse, kv_all, kv_all_t, hidden_in, x_feat, agg_msg, adjacency_t, slots, w_msg, w_self, w_q_t, w_k_t, w_v_t, w_o, pre_act, y_cot, w_up, w_down)
        grad_k, grad_v = grad_kv[:head_dim].T, grad_kv[head_dim:].T
        return (y_out, dx_feat, grad_msg, grad_self, grad_q, grad_k, grad_v, grad_o, grad_up, grad_down)

    return jax.shard_map(device_step, mesh=mesh, in_specs=(row_spec, flat_spec, halo_spec, row_spec, row_spec, row_spec, flat_spec, row_spec, row_spec) + (P(),) * 8, out_specs=(row_spec, row_spec) + (grad_spec,) * 8, check_vma=False)
```

time: 334 us -> 315 us (0.943)
  matrix products: 30 us -> 0 us
  Pallas kernels: 272 us -> 283 us
    dot_general x8 -> x0, matrix products: 30 us -> none  [dot(): return lax.dot_general(a, b, dims, preferred_element_type=F32)]
    pallas_call x1, Pallas kernels: 165 us -> 176 us  [backward(): pl.pallas_call(functools.partial(backward_kernel, head_dim, q_block, key_...]
    unnamed x62 -> x51, local copies, waits for them, and re-layouts: 26.3 us -> 27.2 us
where the time goes in v1:
time: 315 us; the launch traced here: 314 us
  Pallas kernels  283 us (90%)
  local copies, waits for them, and re-layouts  29.9 us (9%)
    pallas_call x1, Pallas kernels, backward(): pl.pallas_call(functools.partial(backward_kernel, head_dim, q_block, key_...  176 us
    pallas_call x1, Pallas kernels, front(): pl.pallas_call(front_kernel, out_shape=[jax.ShapeDtypeStruct(shape, dtype...  54.5 us
    pallas_call x1, Pallas kernels, attention_forward(): pl.pallas_call(functools.partial(attention_fwd_kernel, head_dim, q_block,...  52 us
    unnamed x51, local copies, waits for them, and re-layouts  27.2 us

profile of v1, /device:TPU:0, one launch (start us, length us, event | category | flops | bytes accessed | tf_op | source)
XLA Modules:
  0.0 314.3 jit_solution(16117244116991293351)
XLA Ops:
  0.7 0.1 pad.3.clone
  0.7 0.7 tile.11
  1.4 0.1 tile.12
  1.5 0.8 add_add_fusion.meta_ref
  2.3 1.3 copy.27
  3.6 0.0 copy-start
  3.6 0.0 copy-start.1
  3.6 1.2 copy-done.1
  4.8 0.0 copy-start.2
  4.8 1.0 copy-done.2
  5.9 0.0 copy-start.3
  5.9 0.8 copy-done.3
  6.7 0.0 copy-start.4
  6.7 0.8 copy-done.4
  7.5 0.0 copy-start.5
  7.5 0.8 copy-done.5
  8.4 0.0 copy-start.6
  8.4 0.8 copy-done.6
  9.2 0.0 copy-start.7
  9.2 0.8 copy-done.7
  10.0 54.5 %front.1 = (bf16[512,1024]{1,0:T(8,128)(2,1)}, bf16[4096,128]{1,0:T(8,128)(2,1)}, bf16[128,4096]{1,0:T(8,128)(2,1)}, bf16[1024,512]{1,0:T(8,128)(2,1)}, bf16[102...) custom-call(s32[8,1024]{1,0:T(8,128)S(1)} %add_add_fusion.meta_ref, ...), custom_call_target="tpu_custom_call" | custom-call | flops 25769803776 | bytes 20971520 | tf_op jit(solution)/shard_map/front/pallas_call | solution.py:211
  64.5 0.0 copy-done
  64.5 0.0 copy-start.13
  64.5 0.0 copy-start.14
  64.5 0.0 copy-start.8
  64.5 1.2 copy-done.8
  65.7 0.0 copy-start.9
  65.8 1.2 copy-done.9
  67.0 0.0 copy-start.10
  67.0 1.2 copy-done.10
  68.2 52.0 %attention_fwd.1 = (bf16[512,1024]{1,0:T(8,128)(2,1)S(1)}, f32[8,1024]{1,0:T(8,128)S(1)}) custom-call(s32[4,512]{1,0:T(4,128)S(1)} %get-tuple-element.30.count_ref, bf16[512,1024]{1,0:T(8,128)(2,1)S(1)} %copy-done.8, bf16[4096,128]{1,0:T(8,128)(2,1)S(1)} %copy-done.9, bf16[128,4096]{1,0:T(8,128)(2,1)S(1)} %copy-done.10), custom_call_target="tpu_custom_call" | custom-call | flops 8589934592 | bytes 4194304 | tf_op jit(solution)/shard_map/attention_fwd/pallas_call | solution.py:297
  120.2 0.0 copy-done.13
  120.2 0.0 copy-done.14
  120.2 0.0 copy-start.11
  120.2 1.0 copy-done.11
  121.2 0.0 copy-start.12
  121.2 0.6 copy-done.12
  121.8 176.3 %backward.1 = (bf16[1024,512]{1,0:T(8,128)(2,1)}, bf16[1024,512]{1,0:T(8,128)(2,1)}, f32[512,2048]{1,0:T(8,128)}, f32[2048,512]{1,0:T(8,128)}, f32[512,512]{1,0:...) custom-call(s32[4,512]{1,0:T(4,128)} %copy-done.13, ...), custom_call_target="tpu_custom_call" | custom-call | flops 21474836480 | bytes 41943040 | tf_op jit(solution)/shard_map/backward/pallas_call | solution.py:658
  298.2 0.0 copy-start.20
  298.2 0.0 copy-start.19
  298.2 1.8 slice_bitcast_fusion
  300.0 0.0 copy-start.18
  300.0 2.4 copy.36
  302.4 0.0 copy-start.17
  302.4 2.4 copy.37
  304.7 0.0 copy-done.20
  304.7 0.0 copy-start.16
  304.7 1.0 copy.38
  305.7 0.0 copy-done.19
  305.7 1.0 copy.39
  306.7 0.0 copy-done.18
  306.7 1.0 copy.40
  307.6 0.0 copy-done.17
  307.6 1.0 copy.41
  308.6 0.0 copy-done.16
  308.6 0.0 copy-start.15
  308.6 2.1 copy.42
  310.7 1.6 copy-done.15
  312.3 2.0 copy.43
  (3 shorter events, 0.0 us)
Async XLA Ops:
  3.6 60.9 %copy-start = (bf16[512,512]{0,1:T(8,128)(2,1)}, bf16[512,512]{0,1:T(8,128)(2,1)S(1)}, u32[]{:S(2)}) copy-start(bf16[512,512]{0,1:T(8,128)(2,1)S(1)} %copy.27) | copy-start | bytes 1572868
  3.6 1.2 copy-start.1
  4.8 1.0 copy-start.2
  5.9 0.8 copy-start.3
  6.7 0.8 copy-start.4
  7.5 0.8 copy-start.5
  8.4 0.8 copy-start.6
  9.2 0.8 copy-start.7
  64.5 55.7 %copy-start.13 = (s32[4,512]{1,0:T(4,128)}, s32[4,512]{1,0:T(4,128)S(1)}, u32[]{:S(2)}) copy-start(s32[4,512]{1,0:T(4,128)S(1)} %get-tuple-element.30.count_ref) | copy-start | bytes 24580
  64.5 55.7 %copy-start.14 = (s32[1,128]{1,0:T(1,128)}, s32[1,128]{1,0:T(1,128)S(1)}, u32[]{:S(2)}) copy-start(s32[1,128]{1,0:T(1,128)S(1)} %get-tuple-element.39.slot_ref) | copy-start | bytes 1540
  64.5 1.2 copy-start.8
  65.7 1.2 copy-start.9
  67.0 1.2 copy-start.10
  120.2 1.0 copy-start.11
  121.2 0.6 copy-start.12
  298.2 6.6 %copy-start.20 = (f32[512,512]{1,0:T(8,128)S(1)}, f32[512,512]{1,0:T(8,128)}, u32[]{:S(2)}) copy-start(f32[512,512]{1,0:T(8,128)} %get-tuple-element.64) | copy-start | bytes 3145732
  298.2 7.5 %copy-start.19 = (f32[512,512]{1,0:T(8,128)S(1)}, f32[512,512]{1,0:T(8,128)}, u32[]{:S(2)}) copy-start(f32[512,512]{1,0:T(8,128)} %get-tuple-element.65) | copy-start | bytes 3145732
  300.0 6.7 %copy-start.18 = (f32[512,512]{1,0:T(8,128)S(1)}, f32[512,512]{1,0:T(8,128)}, u32[]{:S(2)}) copy-start(f32[512,512]{1,0:T(8,128)} %get-tuple-element.66) | copy-start | bytes 3145732
  302.4 5.3 %copy-start.17 = (f32[512,512]{1,0:T(8,128)S(1)}, f32[512,512]{1,0:T(8,128)}, u32[]{:S(2)}) copy-start(f32[512,512]{1,0:T(8,128)} %get-tuple-element.69) | copy-start | bytes 3145732
  304.7 3.9 %copy-start.16 = (f32[512,2048]{1,0:T(8,128)S(1)}, f32[512,2048]{1,0:T(8,128)}, u32[]{:S(2)}) copy-start(f32[512,2048]{1,0:T(8,128)} %get-tuple-element.70) | copy-start | bytes 12582916
  308.6 3.7 %copy-start.15 = (f32[2048,512]{1,0:T(8,128)S(1)}, f32[2048,512]{1,0:T(8,128)}, u32[]{:S(2)}) copy-start(f32[2048,512]{1,0:T(8,128)} %get-tuple-element.71) | copy-start | bytes 12582916

commit v2 on v1

--- a/solution.py
+++ b/solution.py
@@ -43,7 +43,14 @@
 CHUNKS, EDGE_STEP, POS_PIECES, KV_PIECES = 4, 512, 4, 2
 
 
-def front_kernel(meta_ref, x_ref, pos_ref, src_ref, dst_ref, on_ref, w_qt_ref, w_kt_ref, w_vt_ref, w_msg_ref, w_self_ref, q_ref, kv_ref, kvt_ref, hid_ref, agg_ref, pre_ref, adj_ref, slot_ref, count_ref, meta_all, pos_all, pos_acc, counts_acc, edge_acc, halo_out, halo_in, kv_all, meta_send, meta_recv, pos_send, pos_recv, halo_send, halo_recv, kv_send, kv_recv):
+def front_kernel(head_dim, perm_ref, valid_ref, halo_ref, x_hbm, pos_hbm, src_hbm, dst_hbm, on_hbm, w_q_hbm, w_kt_hbm, w_vt_hbm, w_msg_hbm, w_self_hbm, *rest):
+    (out_ref, lse_ref, slot_ref, count_ref), rest = rest[:4], rest[4:]
+    saved, rest = rest[:7], rest[7:]
+    kept, rest = rest[:7], rest[7:]
+    q_ref, kv_ref, kvt_ref, hid_ref, agg_ref, pre_ref, adj_ref = kept
+    loaded, rest = rest[:10], rest[10:]
+    x_ref, pos_ref, src_ref, dst_ref, on_ref, w_q_ref, w_kt_ref, w_vt_ref, w_msg_ref, w_self_ref = loaded
+    w_unit, s_even, s_odd, stat, meta_ref, meta_all, pos_all, pos_acc, counts_acc, edge_acc, halo_out, halo_in, kv_all, load_sem, save_sem, meta_send, meta_recv, pos_send, pos_recv, halo_send, halo_recv, kv_send, kv_recv = rest
     rows_dev, width = x_ref.shape
     table_rows = adj_ref.shape[0]
     half = rows_dev // 2
@@ -51,11 +58,19 @@
     halo_pair = halo_in.shape[1]
     me, chip, side, mate, cross, other = neighbours()
     peers = (mate, cross, other)
+    loads = [pltpu.make_async_copy(src, dst, load_sem.at[i]) for i, (src, dst) in enumerate(zip((x_hbm, pos_hbm, src_hbm, dst_hbm, on_hbm, w_q_hbm, w_kt_hbm, w_vt_hbm, w_msg_hbm, w_self_hbm), loaded))]
+    saves = [pltpu.make_async_copy(src, dst, save_sem.at[i]) for i, (src, dst) in enumerate(zip(kept, saved))]
+    for copy in loads:
+        copy.start()
+    meta_ref[...] = jnp.zeros_like(meta_ref)
+    meta_ref[0:1, :] = perm_ref[...]
+    meta_ref[1:2, :] = valid_ref[...]
+    lanes = nodes * halo_pair
+    mine = lax.broadcasted_iota(jnp.int32, (nodes, lanes), 1) // halo_pair == me
+    meta_ref[2:2 + nodes, 0:lanes] = jnp.where(mine, jnp.concatenate([halo_ref[...]] * nodes, axis=1), -1)
     meet(peers)
 
     meta_copies = [remote(meta_ref, meta_all.at[me], meta_send.at[i], meta_recv.at[me], peer) for i, peer in enumerate(peers)]
-    for copy in meta_copies:
-        copy.start()
     piece = rows_dev // POS_PIECES
 
     def pos_rows(index):
@@ -64,9 +79,14 @@
     pos_to_cross = [remote(pos_ref.at[pos_rows(k), :], pos_all.at[me, pos_rows(k), :], pos_send.at[0, k], pos_recv.at[0, k], cross) for k in range(POS_PIECES)]
     pos_to_mate = [remote(pos_ref.at[pos_rows(k), :], pos_all.at[me, pos_rows(k), :], pos_send.at[1, k], pos_recv.at[1, k], mate) for k in range(POS_PIECES)]
     pos_relay = [remote(pos_all.at[cross, pos_rows(k), :], pos_all.at[cross, pos_rows(k), :], pos_send.at[2, k], pos_recv.at[2, k], mate) for k in range(POS_PIECES)]
+    for copy in meta_copies:
+        copy.start()
+    loads[1].wait()
     for copy in pos_to_cross + pos_to_mate:
         copy.start()
     meta_all[me] = meta_ref[...]
+    for copy in loads[:1] + loads[2:]:
+        copy.wait()
 
     def relay_pos(k):
         pos_to_cross[k].wait_recv()
@@ -158,7 +178,7 @@
 
     hid_ref[...] = (x_ref[...].astype(F32) + pos_acc[...]).astype(BF16)
     kv_all[me] = dot(hid_ref[...], jnp.concatenate([w_kt_ref[...], w_vt_ref[...]], axis=0), NT).astype(BF16)
-    q_ref[...] = dot(w_qt_ref[...], hid_ref[...], NT).astype(BF16)
+    q_ref[...] = dot(w_q_ref[...].T, hid_ref[...], NT).astype(BF16)
     kv_piece = rows_dev // KV_PIECES
 
     def kv_copy(owner, k, kind, peer):
@@ -196,25 +216,41 @@
     for copy in kv_relay:
         copy.wait_recv()
     keep_kv(other)
+    for copy in saves:
+        copy.start()
+    attention_forward(head_dim, rows_dev, count_ref, q_ref, kv_ref, kvt_ref, out_ref, lse_ref, w_unit, s_even, s_odd, stat)
+    for copy in saves:
+        copy.wait()
     for copy in meta_copies + pos_to_cross + pos_to_mate + pos_relay + [halo_copy(peer, me) for peer in peers] + kv_to_cross + kv_to_mate + kv_relay:
         copy.wait_send()
 
 
-def front(meta, x_feat, pos_enc, edge_src, edge_dst, edge_mask, w_q_t, w_k_t, w_v_t, w_msg, w_self, nodes, halo_pair):
+def front(perm, valid, halo_slot, x_feat, pos_enc, edge_src, edge_dst, edge_mask, w_q, w_k_t, w_v_t, w_msg, w_self):
     rows, width = x_feat.shape
-    pair = 2 * w_k_t.shape[0]
+    nodes, halo_pair = halo_slot.shape
+    head_dim = w_k_t.shape[0]
+    pair = 2 * head_dim
+    heads = width // head_dim
     keys = nodes * rows
     table_rows = rows + nodes * halo_pair
     vmem = pl.BlockSpec(memory_space=pltpu.VMEM)
+    anywhere = pl.BlockSpec(memory_space=pl.ANY)
     dma = pltpu.SemaphoreType.DMA
-    out = [((width, rows), BF16), ((keys, pair), BF16), ((pair, keys), BF16), ((rows, width), BF16), ((rows, width), BF16), ((rows, width), F32), ((table_rows, rows), BF16), ((1, nodes * halo_pair), jnp.int32), ((nodes, 512), jnp.int32)]
+    small = [((width, rows), BF16), ((heads, rows), F32), ((1, nodes * halo_pair), jnp.int32), ((nodes, 512), jnp.int32)]
+    saved = [((width, rows), BF16), ((keys, pair), BF16), ((pair, keys), BF16), ((rows, width), BF16), ((rows, width), BF16), ((rows, width), F32), ((table_rows, rows), BF16)]
+    inputs = (x_feat, pos_enc, edge_src, edge_dst, edge_mask, w_q, w_k_t, w_v_t, w_msg, w_self)
     return pl.pallas_call(
-        front_kernel,
-        out_shape=[jax.ShapeDtypeStruct(shape, dtype) for shape, dtype in out],
-        in_specs=[vmem] * 11,
-        out_specs=[vmem] * len(out),
-        scratch_shapes=[
-            pltpu.VMEM((nodes,) + meta.shape, jnp.int32),
+        functools.partial(front_kernel, head_dim),
+        out_shape=[jax.ShapeDtypeStruct(shape, dtype) for shape, dtype in small + saved],
+        in_specs=[vmem] * 3 + [anywhere] * len(inputs),
+        out_specs=[vmem] * len(small) + [anywhere] * len(saved),
+        scratch_shapes=[pltpu.VMEM(shape, dtype) for shape, dtype in saved] + [pltpu.VMEM(a.shape, a.dtype) for a in inputs] + [
+            pltpu.VMEM((pair, Q_BLOCK), BF16),
+            pltpu.VMEM((keys, Q_BLOCK), F32),
+            pltpu.VMEM((keys, Q_BLOCK), F32),
+            pltpu.VMEM((8, Q_BLOCK), F32),
+            pltpu.VMEM((8, rows), jnp.int32),
+            pltpu.VMEM((nodes, 8, rows), jnp.int32),
             pltpu.VMEM((nodes, rows, width), BF16),
             pltpu.VMEM((rows, width), F32),
             pltpu.VMEM((table_rows, rows), F32),
@@ -222,12 +258,12 @@
             pltpu.VMEM((nodes, halo_pair, width), BF16),
             pltpu.VMEM((nodes, halo_pair, width), BF16),
             pltpu.VMEM((nodes, rows, pair), BF16),
-            dma((3,)), dma((nodes,)), dma((3, POS_PIECES)), dma((3, POS_PIECES)), dma((nodes,)), dma((nodes,)), dma((3, KV_PIECES)), dma((3, KV_PIECES)),
+            dma((len(inputs),)), dma((len(saved),)), dma((3,)), dma((nodes,)), dma((3, POS_PIECES)), dma((3, POS_PIECES)), dma((nodes,)), dma((nodes,)), dma((3, KV_PIECES)), dma((3, KV_PIECES)),
         ],
-        compiler_params=pltpu.CompilerParams(vmem_limit_bytes=52 << 20, collective_id=2, has_side_effects=True),
-        cost_estimate=pl.CostEstimate(flops=24 << 30, bytes_accessed=20 << 20, transcendentals=0),
+        compiler_params=pltpu.CompilerParams(vmem_limit_bytes=60 << 20, collective_id=2, has_side_effects=True),
+        cost_estimate=pl.CostEstimate(flops=24 << 30, bytes_accessed=20 << 20, transcendentals=heads * rows * keys),
         name='front',
-    )(meta, x_feat, pos_enc, edge_src, edge_dst, edge_mask, w_q_t, w_k_t, w_v_t, w_msg, w_self)
+    )(perm, valid, halo_slot, *inputs)
 
 
 def mask_tail(scores, chunk, key_chunk, part_rows, count_ref):
@@ -239,71 +275,59 @@
     return jnp.concatenate([scores[:key_chunk - TAIL, :], tail], axis=0)
 
 
-def attention_fwd_kernel(head_dim, q_block, key_chunk, part_rows, count_ref, q_ref, kv_ref, kvt_ref, out_ref, lse_ref, w_q, s_buf, stat):
+Q_BLOCK, KEY_CHUNK = 256, 1024
+
+
+def attention_forward(head_dim, part_rows, count_ref, q_ref, kv_ref, kvt_ref, out_ref, lse_ref, w_q, s_even, s_odd, stat):
     heads = q_ref.shape[0] // head_dim
-    blocks = q_ref.shape[1] // q_block
+    blocks = q_ref.shape[1] // Q_BLOCK
     units = heads * blocks
-    keys = kv_ref.shape[0]
-    chunks = keys // key_chunk
+    chunks = kv_ref.shape[0] // KEY_CHUNK
     factor = head_dim ** -0.5 * LOG2E
-    groups = key_chunk // 8
+    groups = KEY_CHUNK // 8
 
     def load_weights(unit):
         head, block = unit // blocks, lax.rem(unit, blocks)
-        w_q[:head_dim, :] = q_ref[pl.ds(pl.multiple_of(head * head_dim, head_dim), head_dim), pl.ds(pl.multiple_of(block * q_block, q_block), q_block)]
-
-    def score_stage(slot, chunk, run_max):
-        rows = pl.ds(pl.multiple_of(chunk * key_chunk, key_chunk), key_chunk)
-        scores = mask_tail(dot(kv_ref[rows, :], w_q[...]), chunk, key_chunk, part_rows, count_ref)
-        s_buf[slot, rows, :] = scores
-        return jnp.maximum(run_max, jnp.max(scores.reshape(groups, 8, q_block), axis=0))
-
-    w_q[head_dim:, :] = jnp.zeros((w_q.shape[0] - head_dim, q_block), BF16)
-    floor = jnp.full((8, q_block), -jnp.inf, F32)
+        w_q[:head_dim, :] = q_ref[pl.ds(pl.multiple_of(head * head_dim, head_dim), head_dim), pl.ds(pl.multiple_of(block * Q_BLOCK, Q_BLOCK), Q_BLOCK)]
+
+    def score_stage(buffer, chunk, run_max):
+        rows = pl.ds(pl.multiple_of(chunk * KEY_CHUNK, KEY_CHUNK), KEY_CHUNK)
+        scores = mask_tail(dot(kv_ref[rows, :], w_q[...]), chunk, KEY_CHUNK, part_rows, count_ref)
+        buffer[rows, :] = scores
+        return jnp.maximum(run_max, jnp.max(scores.reshape(groups, 8, Q_BLOCK), axis=0))
+
+    w_q[head_dim:, :] = jnp.zeros((w_q.shape[0] - head_dim, Q_BLOCK), BF16)
+    floor = jnp.full((8, Q_BLOCK), -jnp.inf, F32)
     load_weights(0)
-    stat[...] = lax.fori_loop(0, chunks, lambda chunk, run_max: score_stage(0, chunk, run_max), floor)
-
-    def unit_body(unit, carry):
-        slot = lax.rem(unit, 2)
+    stat[...] = lax.fori_loop(0, chunks, lambda chunk, run_max: score_stage(s_even, chunk, run_max), floor)
+
+    def one_unit(unit, held, free):
         load_weights(jnp.minimum(unit + 1, units - 1))
         top = jnp.max(stat[...], axis=0, keepdims=True) * factor
 
         def chunk_body(chunk, state):
             run_max, run_sum, weighted = state
-            cols = pl.ds(pl.multiple_of(chunk * key_chunk, key_chunk), key_chunk)
-            prob = jnp.exp2(s_buf[slot, cols, :] * factor - top)
-            run_sum = run_sum + jnp.sum(prob.reshape(groups, 8, q_block), axis=0)
+            cols = pl.ds(pl.multiple_of(chunk * KEY_CHUNK, KEY_CHUNK), KEY_CHUNK)
+            run_max = score_stage(free, chunk, run_max)
+            prob = jnp.exp2(held[cols, :] * factor - top)
+            run_sum = run_sum + jnp.sum(prob.reshape(groups, 8, Q_BLOCK), axis=0)
             weighted = weighted + dot(kvt_ref[head_dim:2 * head_dim, cols], prob.astype(BF16))
-            return score_stage(1 - slot, chunk, run_max), run_sum, weighted
-
-        run_max, run_sum, weighted = lax.fori_loop(0, chunks, chunk_body, (floor, jnp.zeros((8, q_block), F32), jnp.zeros((head_dim, q_block), F32)))
+            return run_max, run_sum, weighted
+
+        run_max, run_sum, weighted = lax.fori_loop(0, chunks, chunk_body, (floor, jnp.zeros((8, Q_BLOCK), F32), jnp.zeros((head_dim, Q_BLOCK), F32)))
         stat[...] = run_max
         total = jnp.sum(run_sum, axis=0, keepdims=True)
         head, block = unit // blocks, lax.rem(unit, blocks)
-        cols = pl.ds(pl.multiple_of(block * q_block, q_block), q_block)
+        cols = pl.ds(pl.multiple_of(block * Q_BLOCK, Q_BLOCK), Q_BLOCK)
         out_ref[pl.ds(pl.multiple_of(head * head_dim, head_dim), head_dim), cols] = (weighted / total).astype(BF16)
         lse_ref[pl.ds(head, 1), cols] = top + jnp.log2(total)
+
+    def unit_pair(pair, carry):
+        one_unit(2 * pair, s_even, s_odd)
+        one_unit(2 * pair + 1, s_odd, s_even)
         return carry
 
-    lax.fori_loop(0, units, unit_body, 0)
-
-
-def attention_forward(counts, q_t, kv, kv_t, head_dim, part_rows):
-    width, rows = q_t.shape
-    keys = kv.shape[0]
-    heads = width // head_dim
-    q_block, key_chunk = 256, 1024
-    vmem = pl.BlockSpec(memory_space=pltpu.VMEM)
-    return pl.pallas_call(
-        functools.partial(attention_fwd_kernel, head_dim, q_block, key_chunk, part_rows),
-        out_shape=[jax.ShapeDtypeStruct((width, rows), BF16), jax.ShapeDtypeStruct((heads, rows), F32)],
-        in_specs=[vmem] * 4,
-        out_specs=[vmem, vmem],
-        scratch_shapes=[pltpu.VMEM((2 * head_dim, q_block), BF16), pltpu.VMEM((2, keys, q_block), F32), pltpu.VMEM((8, q_block), F32)],
-        compiler_params=pltpu.CompilerParams(vmem_limit_bytes=48 << 20),
-        cost_estimate=pl.CostEstimate(flops=4 * heads * rows * keys * head_dim, bytes_accessed=4 << 20, transcendentals=heads * rows * keys),
-        name='attention_fwd',
-    )(counts, q_t, kv, kv_t)
+    lax.fori_loop(0, units // 2, unit_pair, 0)
 
 
 FINAL_STEPS, FINAL_LAG = 14, 1
@@ -312,10 +336,13 @@
 GELU_A, GELU_B = math.sqrt(2.0 / math.pi), 0.044715
 
 
-def backward_kernel(head_dim, q_block, key_chunk, part_rows, count_ref, q_ref, o_ref, lse_ref, kv_ref, kvt_ref, hid_ref, x_ref, agg_ref, adj_ref, slot_ref, w_msg_ref, w_self_ref, w_qt_ref, w_kt_ref, w_vt_ref, w_o_ref, pre_hbm, cot_hbm, up_hbm, down_hbm, *rest):
+def backward_kernel(head_dim, q_block, key_chunk, part_rows, count_ref, o_ref, lse_ref, slot_ref, x_ref, w_o_ref, pre_hbm, cot_hbm, up_hbm, down_hbm, *rest):
+    later, rest = rest[:10], rest[10:]
     y_ref, dx_ref, rest = rest[0], rest[1], rest[2:]
     sum_refs, kv_sum_ref, rest = rest[:6], rest[6], rest[7:]
-    do_buf, dz_buf, dpre_buf, dx_acc, dkv_in, dkv_sum, local, from_mate, from_cross, kv_local, kv_own, kv_in, halo_out, halo_in, load_sem, keep_sem, send_sem, recv_sem, dkv_send, dkv_recv, kv_sem, kv_send, kv_recv, halo_send, halo_recv = rest
+    held, rest = rest[:10], rest[10:]
+    q_ref, kv_ref, kvt_ref, hid_ref, agg_ref, adj_ref, w_msg_ref, w_self_ref, w_q_ref, w_kvt_ref = held
+    do_buf, dz_buf, dpre_buf, dx_acc, dkv_in, dkv_sum, local, from_mate, from_cross, kv_local, kv_own, kv_in, halo_out, halo_in, load_sem, held_sem, keep_sem, send_sem, recv_sem, dkv_send, dkv_recv, kv_sem, kv_send, kv_recv, halo_send, halo_recv = rest
     heads = q_ref.shape[0] // head_dim
     blocks = q_ref.shape[1] // q_block
     units = heads * blocks
@@ -388,9 +415,11 @@
     def halo_copy(peer, owner):
         return remote(halo_out.at[peer], halo_in.at[owner], halo_send.at[peer], halo_recv.at[owner], peer)
 
+    held_loads = [pltpu.make_async_copy(src, dst, held_sem.at[i]) for i, (src, dst) in enumerate(zip(later, held))]
+
     def ffn_phase(w_up, w_down, g_buf, z_buf, y_acc, act, d_act):
         loads = [pltpu.make_async_copy(src, dst, load_sem.at[i]) for i, (src, dst) in enumerate(((pre_hbm, dx_acc), (cot_hbm, g_buf), (up_hbm, w_up), (down_hbm, w_down)))]
-        for copy in loads:
+        for copy in loads + held_loads:
             copy.start()
         meet((mate, cross, other))
         y_acc[...] = dot(o_ref[...], w_o_ref[...], TN)
@@ -449,6 +478,8 @@
         y_ref[...] = jnp.where(keep, y_acc[...], 0.0).astype(BF16)
 
     pl.run_scoped(ffn_phase, pltpu.VMEM(up_hbm.shape, BF16), pltpu.VMEM(down_hbm.shape, BF16), pltpu.VMEM(x_ref.shape, BF16), pltpu.VMEM(x_ref.shape, BF16), pltpu.VMEM(x_ref.shape, F32), pltpu.VMEM(x_ref.shape, BF16), pltpu.VMEM(x_ref.shape, BF16))
+    for copy in held_loads:
+        copy.wait()
     d_z = dx_acc[...].astype(BF16)
     dz_buf[...] = d_z
     dpre_buf[...] = jnp.where(dpre_buf[...] > 0, d_z, jnp.zeros_like(d_z))
@@ -593,7 +624,7 @@
         dkv = jnp.where(lane < head_dim, dkv * scale, dkv).astype(BF16)
         mate_copy(last).start()
         kv_local[...] = dot(dkv, hid_ref[...], TN)
-        dx_acc[...] += dot(dkv, jnp.concatenate([w_kt_ref[...], w_vt_ref[...]], axis=0))
+        dx_acc[...] += dot(dkv, w_kvt_ref[...])
         kv_to_mate.start()
         chip_sum(last)
         kv_to_mate.wait_recv()
@@ -604,7 +635,7 @@
         dx_acc[...] += dot(slot_hot, halo_in[...].reshape(4 * halo_pair, width))
         cross_copy(last).start()
         kv_to_cross.start()
-        dx_ref[...] = (dx_acc[...] + dot(dq_all[...], w_qt_ref[...], TN)).astype(BF16)
+        dx_ref[...] = (dx_acc[...] + dot(dq_all[...], w_q_ref[...].T, TN)).astype(BF16)
         for index in range(done, total):
             group_sum(index)
             if index > done:
@@ -641,7 +672,7 @@
         back_copy(index, 1 - side).wait_recv()
 
 
-def backward(counts, q_t, o_t, lse, kv, kv_t, hidden_in, x_feat, agg_msg, adjacency_t, slots, w_msg, w_self, w_q_t, w_k_t, w_v_t, w_o, pre_act, y_cot, w_up, w_down):
+def backward(counts, o_t, lse, slots, x_feat, w_o, pre_act, y_cot, w_up, w_down, q_t, kv, kv_t, hidden_in, agg_msg, adjacency_t, w_msg, w_self, w_q, w_kv_t):
     width, rows = q_t.shape
     keys = kv.shape[0]
     head_dim = kv.shape[1] // 2
@@ -652,15 +683,16 @@
     shapes = [w_up.shape, w_down.shape] + [(width, width)] * 4
     total = sum(r * c // (width * width) for r, c in shapes)
     halo_pair = slots.shape[1] // nodes
+    later = (q_t, kv, kv_t, hidden_in, agg_msg, adjacency_t, w_msg, w_self, w_q, w_kv_t)
     vmem = pl.BlockSpec(memory_space=pltpu.VMEM)
     anywhere = pl.BlockSpec(memory_space=pl.ANY)
     dma = pltpu.SemaphoreType.DMA
     return pl.pallas_call(
         functools.partial(backward_kernel, head_dim, q_block, key_chunk, rows),
         out_shape=[jax.ShapeDtypeStruct((rows, width), BF16)] * 2 + [jax.ShapeDtypeStruct(shape, F32) for shape in shapes] + [jax.ShapeDtypeStruct((2 * head_dim, width), F32)],
-        in_specs=[vmem] * 17 + [anywhere] * 4,
+        in_specs=[vmem] * 6 + [anywhere] * 14,
         out_specs=[vmem] * 2 + [anywhere] * 7,
-        scratch_shapes=[
+        scratch_shapes=[pltpu.VMEM(a.shape, a.dtype) for a in later] + [
             pltpu.VMEM((width, rows), BF16),
             pltpu.VMEM((rows, width), BF16),
             pltpu.VMEM((rows, width), BF16),
@@ -675,12 +707,12 @@
             pltpu.VMEM((2, head_dim, width), F32),
             pltpu.VMEM((nodes, halo_pair, width), BF16),
             pltpu.VMEM((nodes, halo_pair, width), BF16),
-            dma((4,)), dma((total,)), dma((3, total)), dma((3, total)), dma((3,)), dma((3,)), dma, dma((3,)), dma((3,)), dma((nodes,)), dma((nodes,)),
+            dma((4,)), dma((len(later),)), dma((total,)), dma((3, total)), dma((3, total)), dma((3,)), dma((3,)), dma, dma((3,)), dma((3,)), dma((nodes,)), dma((nodes,)),
         ],
         compiler_params=pltpu.CompilerParams(vmem_limit_bytes=67043328, collective_id=1, has_side_effects=True),
         cost_estimate=pl.CostEstimate(flops=10 * heads * rows * keys * head_dim, bytes_accessed=40 << 20, transcendentals=heads * rows * keys),
         name='backward',
-    )(counts, q_t, o_t, lse, kv, kv_t, hidden_in, x_feat, agg_msg, adjacency_t, slots, w_msg, w_self, w_q_t, w_k_t, w_v_t, w_o, pre_act, y_cot, w_up, w_down)
+    )(counts, o_t, lse, slots, x_feat, w_o, pre_act, y_cot, w_up, w_down, *later)
 
 
 def solution(mesh):
@@ -691,18 +723,10 @@
     grad_spec = P('graphs', None)
 
     def device_step(x_feat, valid, halo_slot, edge_src, edge_dst, edge_mask, bal_perm, pos_enc, y_cot, w_msg, w_self, w_q, w_k, w_v, w_o, w_up, w_down):
-        rows_dev, width = x_feat.shape
         head_dim = w_k.shape[1]
-        me = lax.axis_index('nodes')
-        halo_pair = halo_slot.shape[2]
-
-        lane_owner = jnp.arange(rows_dev)[None, :] // halo_pair
-        wanted = jnp.where(lane_owner == me, jnp.tile(halo_slot.reshape(nodes, halo_pair), (1, rows_dev // halo_pair)), -1)
-        meta = jnp.concatenate([bal_perm[None, :], valid[None, :], wanted, jnp.zeros((6 - nodes, rows_dev), jnp.int32)], axis=0)
-        w_q_t, w_k_t, w_v_t = w_q.T, w_k.T, w_v.T
-        q_t, kv_all, kv_all_t, hidden_in, agg_msg, pre_act, adjacency_t, slots, counts = front(meta, x_feat, pos_enc, edge_src, edge_dst, edge_mask, w_q_t, w_k_t, w_v_t, w_msg, w_self, nodes, halo_pair)
-        mixed_t, lse = attention_forward(counts, q_t, kv_all, kv_all_t, head_dim, rows_dev)
-        y_out, dx_feat, grad_up, grad_down, grad_self, grad_msg, grad_o, grad_q, grad_kv = backward(counts, q_t, mixed_t, lse, kv_all, kv_all_t, hidden_in, x_feat, agg_msg, adjacency_t, slots, w_msg, w_self, w_q_t, w_k_t, w_v_t, w_o, pre_act, y_cot, w_up, w_down)
+        mixed_t, lse, slots, counts, q_t, kv, kv_t, hidden_in, agg_msg, pre_act, adjacency_t = front(bal_perm[None, :], valid[None, :], halo_slot.reshape(nodes, -1), x_feat, pos_enc, edge_src, edge_dst, edge_mask, w_q, w_k.T, w_v.T, w_msg, w_self)
+        w_kv_t = jnp.concatenate([w_k.T, w_v.T], axis=0)
+        y_out, dx_feat, grad_up, grad_down, grad_self, grad_msg, grad_o, grad_q, grad_kv = backward(counts, mixed_t, lse, slots, x_feat, w_o, pre_act, y_cot, w_up, w_down, q_t, kv, kv_t, hidden_in, agg_msg, adjacency_t, w_msg, w_self, w_q, w_kv_t)
         grad_k, grad_v = grad_kv[:head_dim].T, grad_kv[head_dim:].T
         return (y_out, dx_feat, grad_msg, grad_self, grad_q, grad_k, grad_v, grad_o, grad_up, grad_down)
 

time: 315 us -> 297 us (0.943)
  local copies, waits for them, and re-layouts: 29.9 us -> 16.1 us
  Pallas kernels: 283 us -> 279 us
    unnamed x51 -> x20, local copies, waits for them, and re-layouts: 27.2 us -> 14.3 us
    pallas_call x2 -> x1, Pallas kernels: 106 us -> 104 us  [front(): pl.pallas_call(functools.partial(front_kernel, head_dim), out_shape=[jax....]
where the time goes in v2:
time: 297 us
  Pallas kernels  279 us (94%)
  local copies, waits for them, and re-layouts  16.1 us (5%)
    pallas_call x1, Pallas kernels, backward(): pl.pallas_call(functools.partial(backward_kernel, head_dim, q_block, key_...  175 us
    pallas_call x1, Pallas kernels, front(): pl.pallas_call(functools.partial(front_kernel, head_dim), out_shape=[jax....  104 us
    unnamed x20, local copies, waits for them, and re-layouts  14.3 us

profile of v2, /device:TPU:0, one launch (start us, length us, event | category | flops | bytes accessed | tf_op | source)
XLA Modules:
  0.0 297.1 jit_solution(5012241741731971792)
XLA Ops:
  0.6 1.5 pad_maximum_fusion.rest_9_
  2.2 104.2 %front.1 = (bf16[512,1024]{1,0:T(8,128)(2,1)}, f32[8,1024]{1,0:T(8,128)}, s32[1,128]{1,0:T(1,128)}, s32[4,512]{1,0:T(4,128)}, bf16[512,1024]{1,0:T(8,128)(2,1)},...) custom-call(s32[1,1024]{1,0:T(1,128)} %bitcast.13, ...), custom_call_target="tpu_custom_call" | custom-call | flops 25769803776 | bytes 20971520 | tf_op jit(solution)/shard_map/front/pallas_call | solution.py:242
  106.4 174.6 %backward.1 = (bf16[1024,512]{1,0:T(8,128)(2,1)}, bf16[1024,512]{1,0:T(8,128)(2,1)}, f32[512,2048]{1,0:T(8,128)}, f32[2048,512]{1,0:T(8,128)}, f32[512,512]{1,0:...) custom-call(s32[4,512]{1,0:T(4,128)} %get-tuple-element.30.count_ref, ...), custom_call_target="tpu_custom_call" | custom-call | flops 21474836480 | bytes 41943040 | tf_op jit(solution)/shard_map/backward/pallas_call | solution.py:690
  280.9 0.0 copy-start.5
  281.0 0.0 copy-start.4
  281.0 1.8 slice_bitcast_fusion
  282.8 0.0 copy-start.3
  282.8 2.4 copy.35
  285.1 0.0 copy-start.2
  285.1 2.4 copy.36
  287.5 0.0 copy-done.5
  287.5 0.0 copy-start.1
  287.5 1.0 copy.37
  288.5 0.0 copy-done.4
  288.5 1.0 copy.38
  289.4 0.0 copy-done.3
  289.5 1.0 copy.39
  290.4 0.0 copy-done.2
  290.4 1.0 copy.40
  291.4 0.0 copy-done.1
  291.4 0.0 copy-start
  291.4 2.1 copy.41
  293.5 1.6 copy-done
  295.1 2.0 copy.42
Async XLA Ops:
  280.9 6.6 %copy-start.5 = (f32[512,512]{1,0:T(8,128)S(1)}, f32[512,512]{1,0:T(8,128)}, u32[]{:S(2)}) copy-start(f32[512,512]{1,0:T(8,128)} %get-tuple-element.64) | copy-start | bytes 3145732
  281.0 7.5 %copy-start.4 = (f32[512,512]{1,0:T(8,128)S(1)}, f32[512,512]{1,0:T(8,128)}, u32[]{:S(2)}) copy-start(f32[512,512]{1,0:T(8,128)} %get-tuple-element.65) | copy-start | bytes 3145732
  282.8 6.7 %copy-start.3 = (f32[512,512]{1,0:T(8,128)S(1)}, f32[512,512]{1,0:T(8,128)}, u32[]{:S(2)}) copy-start(f32[512,512]{1,0:T(8,128)} %get-tuple-element.66) | copy-start | bytes 3145732
  285.1 5.3 %copy-start.2 = (f32[512,512]{1,0:T(8,128)S(1)}, f32[512,512]{1,0:T(8,128)}, u32[]{:S(2)}) copy-start(f32[512,512]{1,0:T(8,128)} %get-tuple-element.69) | copy-start | bytes 3145732
  287.5 3.9 %copy-start.1 = (f32[512,2048]{1,0:T(8,128)S(1)}, f32[512,2048]{1,0:T(8,128)}, u32[]{:S(2)}) copy-start(f32[512,2048]{1,0:T(8,128)} %get-tuple-element.70) | copy-start | bytes 12582916
  291.4 3.7 %copy-start = (f32[2048,512]{1,0:T(8,128)S(1)}, f32[2048,512]{1,0:T(8,128)}, u32[]{:S(2)}) copy-start(f32[2048,512]{1,0:T(8,128)} %get-tuple-element.71) | copy-start | bytes 12582916

commit v3 on v2

--- a/solution.py
+++ b/solution.py
@@ -62,12 +62,14 @@
     saves = [pltpu.make_async_copy(src, dst, save_sem.at[i]) for i, (src, dst) in enumerate(zip(kept, saved))]
     for copy in loads:
         copy.start()
-    meta_ref[...] = jnp.zeros_like(meta_ref)
+    lanes = nodes * halo_pair
+    assert (nodes + 1) * lanes <= rows_dev
     meta_ref[0:1, :] = perm_ref[...]
-    meta_ref[1:2, :] = valid_ref[...]
-    lanes = nodes * halo_pair
-    mine = lax.broadcasted_iota(jnp.int32, (nodes, lanes), 1) // halo_pair == me
-    meta_ref[2:2 + nodes, 0:lanes] = jnp.where(mine, jnp.concatenate([halo_ref[...]] * nodes, axis=1), -1)
+    mine = lax.broadcasted_iota(jnp.int32, (1, lanes), 1) // halo_pair == me
+    for owner in range(nodes):
+        meta_ref[1:2, owner * lanes:(owner + 1) * lanes] = jnp.where(mine, jnp.concatenate([halo_ref[owner:owner + 1, :]] * nodes, axis=1), -1)
+    held = jnp.sum(valid_ref[...].astype(F32), axis=1, keepdims=True).astype(jnp.int32)
+    meta_ref[1:2, nodes * lanes:] = jnp.broadcast_to(held, (1, rows_dev - nodes * lanes))
     meet(peers)
 
     meta_copies = [remote(meta_ref, meta_all.at[me], meta_send.at[i], meta_recv.at[me], peer) for i, peer in enumerate(peers)]
@@ -146,11 +148,10 @@
     count_chunk(0)
     for peer in peers:
         remote(meta_ref, meta_all.at[peer], meta_send.at[0], meta_recv.at[peer], peer).wait_recv()
-    tables = meta_all[0, :, 0:nodes * halo_pair]
-    for node in range(1, nodes):
-        tables = jnp.maximum(tables, meta_all[node, :, 0:nodes * halo_pair])
-    tables = jnp.where(lax.broadcasted_iota(jnp.int32, tables.shape, 0) == 2 + me, tables, -1)
-    slots = jnp.max(tables.astype(F32), axis=0, keepdims=True).astype(jnp.int32)
+    slots = jnp.full((1, lanes), -1, jnp.int32)
+    for node in range(nodes):
+        for owner in range(nodes):
+            slots = jnp.maximum(slots, jnp.where(me == owner, meta_all[node, 1:2, owner * lanes:(owner + 1) * lanes], -1))
     slot_ref[...] = slots
     slot_hot = jnp.where(lax.broadcasted_iota(jnp.int32, (rows_dev, nodes * halo_pair), 0) == slots, 1.0, 0.0).astype(BF16)
     halo_out[...] = dot(slot_hot, x_ref[...], TN).astype(BF16).reshape(halo_out.shape)
@@ -160,8 +161,7 @@
         halo_copy(peer, me).start()
     halo_in[me] = halo_out[me]
     for node in range(nodes):
-        held = jnp.sum(meta_all[node, 1:2, :].astype(F32), axis=1, keepdims=True).astype(jnp.int32)
-        count_ref[node:node + 1, :] = jnp.broadcast_to(held, (1, count_ref.shape[1]))
+        count_ref[node:node + 1, :] = meta_all[node, 1:2, nodes * lanes:]
     count_chunk(1)
     relay_pos(1)
     for copy in pos_to_mate:
@@ -236,7 +236,7 @@
     vmem = pl.BlockSpec(memory_space=pltpu.VMEM)
     anywhere = pl.BlockSpec(memory_space=pl.ANY)
     dma = pltpu.SemaphoreType.DMA
-    small = [((width, rows), BF16), ((heads, rows), F32), ((1, nodes * halo_pair), jnp.int32), ((nodes, 512), jnp.int32)]
+    small = [((width, rows), BF16), ((heads, rows), F32), ((1, nodes * halo_pair), jnp.int32), ((nodes, rows - nodes * nodes * halo_pair), jnp.int32)]
     saved = [((width, rows), BF16), ((keys, pair), BF16), ((pair, keys), BF16), ((rows, width), BF16), ((rows, width), BF16), ((rows, width), F32), ((table_rows, rows), BF16)]
     inputs = (x_feat, pos_enc, edge_src, edge_dst, edge_mask, w_q, w_k_t, w_v_t, w_msg, w_self)
     return pl.pallas_call(
@@ -249,8 +249,8 @@
             pltpu.VMEM((keys, Q_BLOCK), F32),
             pltpu.VMEM((keys, Q_BLOCK), F32),
             pltpu.VMEM((8, Q_BLOCK), F32),
-            pltpu.VMEM((8, rows), jnp.int32),
-            pltpu.VMEM((nodes, 8, rows), jnp.int32),
+            pltpu.VMEM((2, rows), jnp.int32),
+            pltpu.VMEM((nodes, 2, rows), jnp.int32),
             pltpu.VMEM((nodes, rows, width), BF16),
             pltpu.VMEM((rows, width), F32),
             pltpu.VMEM((table_rows, rows), F32),
@@ -337,11 +337,14 @@
 
 
 def backward_kernel(head_dim, q_block, key_chunk, part_rows, count_ref, o_ref, lse_ref, slot_ref, x_ref, w_o_ref, pre_hbm, cot_hbm, up_hbm, down_hbm, *rest):
-    later, rest = rest[:10], rest[10:]
-    y_ref, dx_ref, rest = rest[0], rest[1], rest[2:]
+    later, rest = rest[:11], rest[11:]
+    row_outs, rest = rest[:2], rest[2:]
     sum_refs, kv_sum_ref, rest = rest[:6], rest[6], rest[7:]
-    held, rest = rest[:10], rest[10:]
-    q_ref, kv_ref, kvt_ref, hid_ref, agg_ref, adj_ref, w_msg_ref, w_self_ref, w_q_ref, w_kvt_ref = held
+    held, rest = rest[:11], rest[11:]
+    (y_ref, dx_ref), rest = rest[:2], rest[2:]
+    row_copies = [pltpu.make_async_copy(src, dst, rest[-1].at[i]) for i, (src, dst) in enumerate(zip((y_ref, dx_ref), row_outs))]
+    rest = rest[:-1]
+    q_ref, kv_ref, kvt_ref, hid_ref, agg_ref, adj_ref, w_msg_ref, w_self_ref, w_q_ref, w_kt_ref, w_vt_ref = held
     do_buf, dz_buf, dpre_buf, dx_acc, dkv_in, dkv_sum, local, from_mate, from_cross, kv_local, kv_own, kv_in, halo_out, halo_in, load_sem, held_sem, keep_sem, send_sem, recv_sem, dkv_send, dkv_recv, kv_sem, kv_send, kv_recv, halo_send, halo_recv = rest
     heads = q_ref.shape[0] // head_dim
     blocks = q_ref.shape[1] // q_block
@@ -419,7 +422,7 @@
 
     def ffn_phase(w_up, w_down, g_buf, z_buf, y_acc, act, d_act):
         loads = [pltpu.make_async_copy(src, dst, load_sem.at[i]) for i, (src, dst) in enumerate(((pre_hbm, dx_acc), (cot_hbm, g_buf), (up_hbm, w_up), (down_hbm, w_down)))]
-        for copy in loads + held_loads:
+        for copy in loads:
             copy.start()
         meet((mate, cross, other))
         y_acc[...] = dot(o_ref[...], w_o_ref[...], TN)
@@ -437,6 +440,8 @@
         y_acc[...] = z_mid.astype(F32)
         loads[2].wait()
         loads[3].wait()
+        for copy in held_loads:
+            copy.start()
 
         def ffn_chunk(chunk, carry):
             cols = pl.ds(pl.multiple_of(chunk * width, width), width)
@@ -478,6 +483,7 @@
         y_ref[...] = jnp.where(keep, y_acc[...], 0.0).astype(BF16)
 
     pl.run_scoped(ffn_phase, pltpu.VMEM(up_hbm.shape, BF16), pltpu.VMEM(down_hbm.shape, BF16), pltpu.VMEM(x_ref.shape, BF16), pltpu.VMEM(x_ref.shape, BF16), pltpu.VMEM(x_ref.shape, F32), pltpu.VMEM(x_ref.shape, BF16), pltpu.VMEM(x_ref.shape, BF16))
+    row_copies[0].start()
     for copy in held_loads:
         copy.wait()
     d_z = dx_acc[...].astype(BF16)
@@ -624,7 +630,7 @@
         dkv = jnp.where(lane < head_dim, dkv * scale, dkv).astype(BF16)
         mate_copy(last).start()
         kv_local[...] = dot(dkv, hid_ref[...], TN)
-        dx_acc[...] += dot(dkv, w_kvt_ref[...])
+        dx_acc[...] += dot(dkv, jnp.concatenate([w_kt_ref[...], w_vt_ref[...]], axis=0))
         kv_to_mate.start()
         chip_sum(last)
         kv_to_mate.wait_recv()
@@ -638,7 +644,9 @@
         dx_ref[...] = (dx_acc[...] + dot(dq_all[...], w_q_ref[...].T, TN)).astype(BF16)
         for index in range(done, total):
             group_sum(index)
-            if index > done:
+            if index == done:
+                row_copies[1].start()
+            else:
                 start_out(index - 1)
         kv_to_cross.wait_recv()
         kv_own[1] = kv_own[0] + kv_in[1]
@@ -662,6 +670,8 @@
     )
     for copy in [kv_to_mate, kv_to_cross, kv_back(side)] + [halo_copy(peer, me) for peer in (mate, cross, other)]:
         copy.wait_send()
+    for copy in row_copies:
+        copy.wait()
     kv_keep.wait()
     kv_back(1 - side).wait_recv()
     for index in range(total):
@@ -672,7 +682,7 @@
         back_copy(index, 1 - side).wait_recv()
 
 
-def backward(counts, o_t, lse, slots, x_feat, w_o, pre_act, y_cot, w_up, w_down, q_t, kv, kv_t, hidden_in, agg_msg, adjacency_t, w_msg, w_self, w_q, w_kv_t):
+def backward(counts, o_t, lse, slots, x_feat, w_o, pre_act, y_cot, w_up, w_down, q_t, kv, kv_t, hidden_in, agg_msg, adjacency_t, w_msg, w_self, w_q, w_k_t, w_v_t):
     width, rows = q_t.shape
     keys = kv.shape[0]
     head_dim = kv.shape[1] // 2
@@ -683,16 +693,18 @@
     shapes = [w_up.shape, w_down.shape] + [(width, width)] * 4
     total = sum(r * c // (width * width) for r, c in shapes)
     halo_pair = slots.shape[1] // nodes
-    later = (q_t, kv, kv_t, hidden_in, agg_msg, adjacency_t, w_msg, w_self, w_q, w_kv_t)
+    later = (q_t, kv, kv_t, hidden_in, agg_msg, adjacency_t, w_msg, w_self, w_q, w_k_t, w_v_t)
     vmem = pl.BlockSpec(memory_space=pltpu.VMEM)
     anywhere = pl.BlockSpec(memory_space=pl.ANY)
     dma = pltpu.SemaphoreType.DMA
     return pl.pallas_call(
         functools.partial(backward_kernel, head_dim, q_block, key_chunk, rows),
         out_shape=[jax.ShapeDtypeStruct((rows, width), BF16)] * 2 + [jax.ShapeDtypeStruct(shape, F32) for shape in shapes] + [jax.ShapeDtypeStruct((2 * head_dim, width), F32)],
-        in_specs=[vmem] * 6 + [anywhere] * 14,
-        out_specs=[vmem] * 2 + [anywhere] * 7,
+        in_specs=[vmem] * 6 + [anywhere] * 15,
+        out_specs=[anywhere] * 9,
         scratch_shapes=[pltpu.VMEM(a.shape, a.dtype) for a in later] + [
+            pltpu.VMEM((rows, width), BF16),
+            pltpu.VMEM((rows, width), BF16),
             pltpu.VMEM((width, rows), BF16),
             pltpu.VMEM((rows, width), BF16),
             pltpu.VMEM((rows, width), BF16),
@@ -707,12 +719,51 @@
             pltpu.VMEM((2, head_dim, width), F32),
             pltpu.VMEM((nodes, halo_pair, width), BF16),
             pltpu.VMEM((nodes, halo_pair, width), BF16),
-            dma((4,)), dma((len(later),)), dma((total,)), dma((3, total)), dma((3, total)), dma((3,)), dma((3,)), dma, dma((3,)), dma((3,)), dma((nodes,)), dma((nodes,)),
+            dma((4,)), dma((len(later),)), dma((total,)), dma((3, total)), dma((3, total)), dma((3,)), dma((3,)), dma, dma((3,)), dma((3,)), dma((nodes,)), dma((nodes,)), dma((2,)),
         ],
         compiler_params=pltpu.CompilerParams(vmem_limit_bytes=67043328, collective_id=1, has_side_effects=True),
         cost_estimate=pl.CostEstimate(flops=10 * heads * rows * keys * head_dim, bytes_accessed=40 << 20, transcendentals=heads * rows * keys),
         name='backward',
     )(counts, o_t, lse, slots, x_feat, w_o, pre_act, y_cot, w_up, w_down, *later)
+
+
+def finish_kernel(plan, *refs):
+    inputs = plan[-1][0] + 1
+    sources, rest = refs[:inputs], refs[inputs:]
+    outputs = plan[-1][1] + 1
+    targets, rest = rest[:outputs], rest[outputs:]
+    buffers, in_sem, out_sem = rest[:-2], rest[-2], rest[-1]
+    gets = [pltpu.make_async_copy(sources[i].at[pl.ds(src, n), :], buf, in_sem.at[k]) for k, ((i, j, src, dst, n), buf) in enumerate(zip(plan, buffers))]
+    puts = [pltpu.make_async_copy(buf, targets[j].at[pl.ds(dst, n), :], out_sem.at[k]) for k, ((i, j, src, dst, n), buf) in enumerate(zip(plan, buffers))]
+    for copy in gets:
+        copy.start()
+    for get, put in zip(gets, puts):
+        get.wait()
+        put.start()
+    for copy in puts:
+        copy.wait()
+
+
+def finish(*arrays):
+    plan, shapes = [], []
+    for i, a in enumerate(arrays):
+        last = i == len(arrays) - 1
+        step = a.shape[0] // 2 if last else min(a.shape[0], (1 << 20) // (a.shape[1] * a.dtype.itemsize))
+        for start in range(0, a.shape[0], step):
+            j = i + (start // step if last else 0)
+            plan.append((i, j, start, 0 if last else start, step))
+        shapes += [jax.ShapeDtypeStruct((step, a.shape[1]), a.dtype)] * 2 if last else [jax.ShapeDtypeStruct(a.shape, a.dtype)]
+    anywhere = pl.BlockSpec(memory_space=pl.ANY)
+    return pl.pallas_call(
+        functools.partial(finish_kernel, plan),
+        out_shape=shapes,
+        in_specs=[anywhere] * len(arrays),
+        out_specs=[anywhere] * len(shapes),
+        scratch_shapes=[pltpu.VMEM((n, arrays[i].shape[1]), arrays[i].dtype) for i, j, src, dst, n in plan] + [pltpu.SemaphoreType.DMA((len(plan),))] * 2,
+        compiler_params=pltpu.CompilerParams(vmem_limit_bytes=67043328),
+        cost_estimate=pl.CostEstimate(flops=1 << 20, bytes_accessed=30 << 20, transcendentals=0),
+        name='finish',
+    )(*arrays)
 
 
 def solution(mesh):
@@ -725,9 +776,8 @@
     def device_step(x_feat, valid, halo_slot, edge_src, edge_dst, edge_mask, bal_perm, pos_enc, y_cot, w_msg, w_self, w_q, w_k, w_v, w_o, w_up, w_down):
         head_dim = w_k.shape[1]
         mixed_t, lse, slots, counts, q_t, kv, kv_t, hidden_in, agg_msg, pre_act, adjacency_t = front(bal_perm[None, :], valid[None, :], halo_slot.reshape(nodes, -1), x_feat, pos_enc, edge_src, edge_dst, edge_mask, w_q, w_k.T, w_v.T, w_msg, w_self)
-        w_kv_t = jnp.concatenate([w_k.T, w_v.T], axis=0)
-        y_out, dx_feat, grad_up, grad_down, grad_self, grad_msg, grad_o, grad_q, grad_kv = backward(counts, mixed_t, lse, slots, x_feat, w_o, pre_act, y_cot, w_up, w_down, q_t, kv, kv_t, hidden_in, agg_msg, adjacency_t, w_msg, w_self, w_q, w_kv_t)
-        grad_k, grad_v = grad_kv[:head_dim].T, grad_kv[head_dim:].T
-        return (y_out, dx_feat, grad_msg, grad_self, grad_q, grad_k, grad_v, grad_o, grad_up, grad_down)
+        results = backward(counts, mixed_t, lse, slots, x_feat, w_o, pre_act, y_cot, w_up, w_down, q_t, kv, kv_t, hidden_in, agg_msg, adjacency_t, w_msg, w_self, w_q, w_k.T, w_v.T)
+        y_out, dx_feat, grad_up, grad_down, grad_self, grad_msg, grad_o, grad_q, grad_k, grad_v = finish(*results)
+        return (y_out, dx_feat, grad_msg, grad_self, grad_q, grad_k.T, grad_v.T, grad_o, grad_up, grad_down)
 
     return jax.shard_map(device_step, mesh=mesh, in_specs=(row_spec, flat_spec, halo_spec, row_spec, row_spec, row_spec, flat_spec, row_spec, row_spec) + (P(),) * 8, out_specs=(row_spec, row_spec) + (grad_spec,) * 8, check_vma=False)

time: 297 us -> 289 us (0.973)
  local copies, waits for them, and re-layouts: 16.1 us -> 0 us
  Pallas kernels: 279 us -> 288 us
    unnamed x20 -> x0, local copies, waits for them, and re-layouts: 14.3 us -> none
    pallas_call x0 -> x1, Pallas kernels: none -> 11.1 us  [finish(): pl.pallas_call(functools.partial(finish_kernel, plan), out_shape=shapes,...]
where the time goes in v3:
time: 289 us; the launch traced here: 288 us
  Pallas kernels  288 us (100%)
    pallas_call x1, Pallas kernels, backward(): pl.pallas_call(functools.partial(backward_kernel, head_dim, q_block, key_...  173 us
    pallas_call x1, Pallas kernels, front(): pl.pallas_call(functools.partial(front_kernel, head_dim), out_shape=[jax....  103 us
    pallas_call x1, Pallas kernels, finish(): pl.pallas_call(functools.partial(finish_kernel, plan), out_shape=shapes,...  11.1 us

profile of v3, /device:TPU:0, one launch (start us, length us, event | category | flops | bytes accessed | tf_op | source)
XLA Modules:
  0.0 288.4 jit_solution(3914694603583382715)
XLA Ops:
  0.6 103.0 %front.1 = (bf16[512,1024]{1,0:T(8,128)(2,1)}, f32[8,1024]{1,0:T(8,128)}, s32[1,128]{1,0:T(1,128)}, s32[4,512]{1,0:T(4,128)}, bf16[512,1024]{1,0:T(8,128)(2,1)},...) custom-call(s32[1,1024]{1,0:T(1,128)} %bitcast.13, ...), custom_call_target="tpu_custom_call" | custom-call | flops 25769803776 | bytes 20971520 | tf_op jit(solution)/shard_map/front/pallas_call | solution.py:242
  103.7 173.5 %backward.1 = (bf16[1024,512]{1,0:T(8,128)(2,1)}, bf16[1024,512]{1,0:T(8,128)(2,1)}, f32[512,2048]{1,0:T(8,128)}, f32[2048,512]{1,0:T(8,128)}, f32[512,512]{1,0:...) custom-call(s32[4,512]{1,0:T(4,128)} %get-tuple-element.40.count_ref, ...), custom_call_target="tpu_custom_call" | custom-call | flops 21474836480 | bytes 41943040 | tf_op jit(solution)/shard_map/backward/pallas_call | solution.py:700
  277.1 11.1 %finish.1 = (bf16[1024,512]{1,0:T(8,128)(2,1)}, bf16[1024,512]{1,0:T(8,128)(2,1)}, f32[512,2048]{1,0:T(8,128)}, f32[2048,512]{1,0:T(8,128)}, f32[512,512]{1,0:T(...) custom-call(bf16[1024,512]{1,0:T(8,128)(2,1)} %get-tuple-element.51., ...), custom_call_target="tpu_custom_call" | custom-call | flops 1048576 | bytes 31457280 | tf_op jit(solution)/shard_map/finish/pallas_call | solution.py:757

commit v4 on v3

--- a/solution.py
+++ b/solution.py
@@ -275,7 +275,7 @@
     return jnp.concatenate([scores[:key_chunk - TAIL, :], tail], axis=0)
 
 
-Q_BLOCK, KEY_CHUNK = 256, 1024
+Q_BLOCK, KEY_CHUNK, UNROLL = 256, 1024, 2
 
 
 def attention_forward(head_dim, part_rows, count_ref, q_ref, kv_ref, kvt_ref, out_ref, lse_ref, w_q, s_even, s_odd, stat):
@@ -305,16 +305,18 @@
         load_weights(jnp.minimum(unit + 1, units - 1))
         top = jnp.max(stat[...], axis=0, keepdims=True) * factor
 
-        def chunk_body(chunk, state):
+        def chunk_body(index, state):
             run_max, run_sum, weighted = state
-            cols = pl.ds(pl.multiple_of(chunk * KEY_CHUNK, KEY_CHUNK), KEY_CHUNK)
-            run_max = score_stage(free, chunk, run_max)
-            prob = jnp.exp2(held[cols, :] * factor - top)
-            run_sum = run_sum + jnp.sum(prob.reshape(groups, 8, Q_BLOCK), axis=0)
-            weighted = weighted + dot(kvt_ref[head_dim:2 * head_dim, cols], prob.astype(BF16))
+            for k in range(UNROLL):
+                chunk = index * UNROLL + k
+                run_max = score_stage(free, chunk, run_max)
+                cols = pl.ds(pl.multiple_of(chunk * KEY_CHUNK, KEY_CHUNK), KEY_CHUNK)
+                prob = jnp.exp2(held[cols, :] * factor - top)
+                run_sum = run_sum + jnp.sum(prob.reshape(groups, 8, Q_BLOCK), axis=0)
+                weighted = weighted + dot(kvt_ref[head_dim:2 * head_dim, cols], prob.astype(BF16))
             return run_max, run_sum, weighted
 
-        run_max, run_sum, weighted = lax.fori_loop(0, chunks, chunk_body, (floor, jnp.zeros((8, Q_BLOCK), F32), jnp.zeros((head_dim, Q_BLOCK), F32)))
+        run_max, run_sum, weighted = lax.fori_loop(0, chunks // UNROLL, chunk_body, (floor, jnp.zeros((8, Q_BLOCK), F32), jnp.zeros((head_dim, Q_BLOCK), F32)))
         stat[...] = run_max
         total = jnp.sum(run_sum, axis=0, keepdims=True)
         head, block = unit // blocks, lax.rem(unit, blocks)
@@ -336,12 +338,12 @@
 GELU_A, GELU_B = math.sqrt(2.0 / math.pi), 0.044715
 
 
-def backward_kernel(head_dim, q_block, key_chunk, part_rows, count_ref, o_ref, lse_ref, slot_ref, x_ref, w_o_ref, pre_hbm, cot_hbm, up_hbm, down_hbm, *rest):
+def backward_kernel(head_dim, q_block, key_chunk, part_rows, count_ref, lse_ref, slot_ref, o_hbm, x_hbm, w_o_hbm, pre_hbm, cot_hbm, up_hbm, down_hbm, *rest):
     later, rest = rest[:11], rest[11:]
     row_outs, rest = rest[:2], rest[2:]
     sum_refs, kv_sum_ref, rest = rest[:6], rest[6], rest[7:]
     held, rest = rest[:11], rest[11:]
-    (y_ref, dx_ref), rest = rest[:2], rest[2:]
+    (y_ref, dx_ref, o_ref, x_ref, w_o_ref), rest = rest[:5], rest[5:]
     row_copies = [pltpu.make_async_copy(src, dst, rest[-1].at[i]) for i, (src, dst) in enumerate(zip((y_ref, dx_ref), row_outs))]
     rest = rest[:-1]
     q_ref, kv_ref, kvt_ref, hid_ref, agg_ref, adj_ref, w_msg_ref, w_self_ref, w_q_ref, w_kt_ref, w_vt_ref = held
@@ -421,62 +423,77 @@
     held_loads = [pltpu.make_async_copy(src, dst, held_sem.at[i]) for i, (src, dst) in enumerate(zip(later, held))]
 
     def ffn_phase(w_up, w_down, g_buf, z_buf, y_acc, act, d_act):
-        loads = [pltpu.make_async_copy(src, dst, load_sem.at[i]) for i, (src, dst) in enumerate(((pre_hbm, dx_acc), (cot_hbm, g_buf), (up_hbm, w_up), (down_hbm, w_down)))]
+        loads = [pltpu.make_async_copy(src, dst, load_sem.at[i]) for i, (src, dst) in enumerate(((o_hbm, o_ref), (w_o_hbm, w_o_ref), (x_hbm, x_ref), (pre_hbm, dx_acc), (cot_hbm, g_buf), (up_hbm, w_up), (down_hbm, w_down)))]
         for copy in loads:
             copy.start()
         meet((mate, cross, other))
+        loads[0].wait()
+        loads[1].wait()
         y_acc[...] = dot(o_ref[...], w_o_ref[...], TN)
-        loads[0].wait()
+        loads[2].wait()
+        loads[3].wait()
         pre = dx_acc[...]
         x_wide = x_ref[...].astype(F32)
         z_mid = (x_wide + jnp.maximum(pre, 0.0) + x_wide + y_acc[...].astype(BF16).astype(F32)).astype(BF16)
         dpre_buf[...] = jnp.where(pre > 0, 1.0, 0.0).astype(BF16)
         z_buf[...] = z_mid
-        loads[1].wait()
+        loads[4].wait()
         keep = lax.broadcasted_iota(jnp.int32, (part_rows, width), 0) < count_ref[pl.ds(me, 1), :width]
         g_wide = jnp.where(keep, g_buf[...].astype(F32), 0.0)
         g_buf[...] = g_wide.astype(BF16)
         dx_acc[...] = g_wide
         y_acc[...] = z_mid.astype(F32)
-        loads[2].wait()
-        loads[3].wait()
-        for copy in held_loads:
-            copy.start()
+        loads[5].wait()
+        loads[6].wait()
 
         def ffn_chunk(chunk, carry):
             cols = pl.ds(pl.multiple_of(chunk * width, width), width)
+
+            def act_block(index, inner):
+                rows = pl.ds(pl.multiple_of(index * ROW_BLOCK, ROW_BLOCK), ROW_BLOCK)
+                h_pre = dot(z_buf[rows, :], w_up[:, cols])
+                bend = jnp.tanh(h_pre * (GELU_A + GELU_A * GELU_B * (h_pre * h_pre)))
+                act[rows, :] = (h_pre * (0.5 + 0.5 * bend)).astype(BF16)
+                return inner
 
             def row_block(index, inner):
                 rows = pl.ds(pl.multiple_of(index * ROW_BLOCK, ROW_BLOCK), ROW_BLOCK)
                 h_pre = dot(z_buf[rows, :], w_up[:, cols])
                 square = h_pre * h_pre
                 bend = jnp.tanh(h_pre * (GELU_A + GELU_A * GELU_B * square))
-                gate = 0.5 + 0.5 * bend
-                act[rows, :] = (h_pre * gate).astype(BF16)
-                slope = gate + (0.5 * h_pre) * (1.0 - bend * bend) * (GELU_A + 3.0 * GELU_A * GELU_B * square)
+                slope = 0.5 + 0.5 * bend + (0.5 * h_pre) * (1.0 - bend * bend) * (GELU_A + 3.0 * GELU_A * GELU_B * square)
                 d_hidden = dot(g_buf[rows, :], w_down[cols, :], NT).astype(BF16)
                 d_act[rows, :] = (d_hidden.astype(F32) * slope).astype(BF16)
                 y_acc[rows, :] += dot(act[rows, :], w_down[cols, :])
                 dx_acc[rows, :] += dot(d_act[rows, :], w_up[:, cols], NT)
                 return inner
 
-            lax.fori_loop(0, part_rows // ROW_BLOCK, row_block, 0)
+            lax.fori_loop(0, part_rows // ROW_BLOCK, act_block, 0)
             local[2 * chunk] = dot(act[...], g_buf[...], TN)
+
+            @pl.when(chunk == 0)
+            def load_later():
+                for copy in held_loads:
+                    copy.start()
 
             @pl.when(chunk > 0)
             def sum_previous():
                 chip_sum(2 * chunk - 1)
 
-            local[2 * chunk + 1] = dot(z_buf[...], d_act[...], TN)
+            row_block(0, 0)
             mate_copy(2 * chunk).start()
 
             @pl.when(chunk > 0)
             def send_previous():
                 cross_copy(2 * chunk - 1).start()
 
+            row_block(1, 0)
             chip_sum(2 * chunk)
+            row_block(2, 0)
+            cross_copy(2 * chunk).start()
+            lax.fori_loop(3, part_rows // ROW_BLOCK, row_block, 0)
+            local[2 * chunk + 1] = dot(z_buf[...], d_act[...], TN)
             mate_copy(2 * chunk + 1).start()
-            cross_copy(2 * chunk).start()
             return carry
 
         lax.fori_loop(0, ffn_chunks, ffn_chunk, 0)
@@ -700,11 +717,14 @@
     return pl.pallas_call(
         functools.partial(backward_kernel, head_dim, q_block, key_chunk, rows),
         out_shape=[jax.ShapeDtypeStruct((rows, width), BF16)] * 2 + [jax.ShapeDtypeStruct(shape, F32) for shape in shapes] + [jax.ShapeDtypeStruct((2 * head_dim, width), F32)],
-        in_specs=[vmem] * 6 + [anywhere] * 15,
+        in_specs=[vmem] * 3 + [anywhere] * 18,
         out_specs=[anywhere] * 9,
         scratch_shapes=[pltpu.VMEM(a.shape, a.dtype) for a in later] + [
             pltpu.VMEM((rows, width), BF16),
             pltpu.VMEM((rows, width), BF16),
+            pltpu.VMEM((width, rows), BF16),
+            pltpu.VMEM((rows, width), BF16),
+            pltpu.VMEM((width, width), BF16),
             pltpu.VMEM((width, rows), BF16),
             pltpu.VMEM((rows, width), BF16),
             pltpu.VMEM((rows, width), BF16),
@@ -719,12 +739,12 @@
             pltpu.VMEM((2, head_dim, width), F32),
             pltpu.VMEM((nodes, halo_pair, width), BF16),
             pltpu.VMEM((nodes, halo_pair, width), BF16),
-            dma((4,)), dma((len(later),)), dma((total,)), dma((3, total)), dma((3, total)), dma((3,)), dma((3,)), dma, dma((3,)), dma((3,)), dma((nodes,)), dma((nodes,)), dma((2,)),
+            dma((7,)), dma((len(later),)), dma((total,)), dma((3, total)), dma((3, total)), dma((3,)), dma((3,)), dma, dma((3,)), dma((3,)), dma((nodes,)), dma((nodes,)), dma((2,)),
         ],
         compiler_params=pltpu.CompilerParams(vmem_limit_bytes=67043328, collective_id=1, has_side_effects=True),
         cost_estimate=pl.CostEstimate(flops=10 * heads * rows * keys * head_dim, bytes_accessed=40 << 20, transcendentals=heads * rows * keys),
         name='backward',
-    )(counts, o_t, lse, slots, x_feat, w_o, pre_act, y_cot, w_up, w_down, *later)
+    )(counts, lse, slots, o_t, x_feat, w_o, pre_act, y_cot, w_up, w_down, *later)
 
 
 def finish_kernel(plan, *refs):

time: 289 us -> 281 us (0.972)
  Pallas kernels: 288 us -> 280 us
    pallas_call x1, Pallas kernels: 103 us -> 94.3 us  [front(): pl.pallas_call(functools.partial(front_kernel, head_dim), out_shape=[jax....]
where the time goes in v4:
time: 281 us
  Pallas kernels  280 us (100%)
    pallas_call x1, Pallas kernels, backward(): pl.pallas_call(functools.partial(backward_kernel, head_dim, q_block, key_...  174 us
    pallas_call x1, Pallas kernels, front(): pl.pallas_call(functools.partial(front_kernel, head_dim), out_shape=[jax....  94.3 us
    pallas_call x1, Pallas kernels, finish(): pl.pallas_call(functools.partial(finish_kernel, plan), out_shape=shapes,...  11.1 us

profile of v4, /device:TPU:0, one launch (start us, length us, event | category | flops | bytes accessed | tf_op | source)
XLA Modules:
  0.0 280.7 jit_solution(12970021619403913084)
XLA Ops:
  0.6 94.3 %front.1 = (bf16[512,1024]{1,0:T(8,128)(2,1)}, f32[8,1024]{1,0:T(8,128)}, s32[1,128]{1,0:T(1,128)}, s32[4,512]{1,0:T(4,128)}, bf16[512,1024]{1,0:T(8,128)(2,1)},...) custom-call(s32[1,1024]{1,0:T(1,128)} %bitcast.13, ...), custom_call_target="tpu_custom_call" | custom-call | flops 25769803776 | bytes 20971520 | tf_op jit(solution)/shard_map/front/pallas_call | solution.py:242
  95.0 174.4 %backward.1 = (bf16[1024,512]{1,0:T(8,128)(2,1)}, bf16[1024,512]{1,0:T(8,128)(2,1)}, f32[512,2048]{1,0:T(8,128)}, f32[2048,512]{1,0:T(8,128)}, f32[512,512]{1,0:...) custom-call(s32[4,512]{1,0:T(4,128)} %get-tuple-element.40.count_ref, ...), custom_call_target="tpu_custom_call" | custom-call | flops 21474836480 | bytes 41943040 | tf_op jit(solution)/shard_map/backward/pallas_call | solution.py:717
  269.4 11.1 %finish.1 = (bf16[1024,512]{1,0:T(8,128)(2,1)}, bf16[1024,512]{1,0:T(8,128)(2,1)}, f32[512,2048]{1,0:T(8,128)}, f32[2048,512]{1,0:T(8,128)}, f32[512,512]{1,0:T(...) custom-call(bf16[1024,512]{1,0:T(8,128)(2,1)} %get-tuple-element.51., ...), custom_call_target="tpu_custom_call" | custom-call | flops 1048576 | bytes 31457280 | tf_op jit(solution)/shard_map/finish/pallas_call | solution.py:777

commit v5 on v4

--- a/solution.py
+++ b/solution.py
@@ -510,18 +510,12 @@
     do_buf[...] = dot(w_o_ref[...], dz_buf[...], NT).astype(BF16)
     cross_copy(first_small - 1).start()
 
-    d_agg = dot(dpre_buf[...], w_msg_ref[...], NT).astype(BF16)
-    halo_out[...] = dot(adj_ref[part_rows:, :], d_agg).astype(BF16).reshape(halo_out.shape)
-    dx_acc[...] = 2.0 * dz_buf[...].astype(F32) + dot(dpre_buf[...], w_self_ref[...], NT)
-    dx_acc[...] += dot(adj_ref[:part_rows, :], d_agg)
-    for peer in (mate, cross, other):
-        halo_copy(peer, me).start()
-    halo_in[me] = halo_out[me]
     local[first_small] = dot(x_ref[...], dpre_buf[...], TN)
     local[first_small + 1] = dot(agg_ref[...], dpre_buf[...], TN)
     local[first_small + 2] = dot(o_ref[...], dz_buf[...])
 
-    def attention_phase(w_q, w_do, lse_buf, delta_buf, p_buf, ds_buf, dq_acc, dq_all, dkv_acc):
+    def attention_phase(w_q_even, w_q_odd, w_do_even, w_do_odd, p_even, p_odd, ds_even, ds_odd, lse_buf, delta_buf, dq_acc, dq_all, dkv_acc):
+        buffers = ((w_q_even, w_do_even, p_even, ds_even), (w_q_odd, w_do_odd, p_odd, ds_odd))
         dkv_copies = [remote(src, dkv_in.at[i], dkv_send.at[i], dkv_recv.at[i], peer) for i, (src, peer) in enumerate(((dkv_acc.at[0], mate), (dkv_sum, cross), (dkv_acc.at[2], mate)))]
 
         def unit_spots(unit):
@@ -536,9 +530,9 @@
             return carry
 
         lax.fori_loop(0, units, prepare, 0)
-        for slot in range(2):
-            w_q[slot, head_dim:, :] = jnp.zeros((head_dim, q_block), BF16)
-            w_do[slot, :head_dim, :] = jnp.zeros((head_dim, q_block), BF16)
+        for w_q, w_do, p_buf, ds_buf in buffers:
+            w_q[head_dim:, :] = jnp.zeros((head_dim, q_block), BF16)
+            w_do[:head_dim, :] = jnp.zeros((head_dim, q_block), BF16)
         dkv_acc[...] = jnp.zeros_like(dkv_acc)
 
         def place_of(step):
@@ -547,27 +541,29 @@
             owner = lax.rem(chip + 1 - group // 2, 2) * 2 + lax.rem(side + 1 - lax.rem(group, 2), 2)
             offset = lax.rem(chunk, halves) * key_chunk
             rows = pl.ds(pl.multiple_of(owner * part_rows + offset, key_chunk), key_chunk)
-            return group, owner, offset, rows, lax.rem(step, units), lax.rem(step, 2)
-
-        def first_stage(step):
-            group, owner, offset, rows, unit, slot = place_of(step)
+            return group, owner, offset, rows, lax.rem(step, units)
+
+        def first_stage(step, parity):
+            w_q, w_do, p_buf, ds_buf = buffers[parity]
+            group, owner, offset, rows, unit = place_of(step)
             head, unit_rows, cols = unit_spots(unit)
-            w_q[slot, :head_dim, :] = q_ref[unit_rows, cols]
-            w_do[slot, head_dim:, :] = do_buf[unit_rows, cols]
+            w_q[:head_dim, :] = q_ref[unit_rows, cols]
+            w_do[head_dim:, :] = do_buf[unit_rows, cols]
             kv = kv_ref[rows, :]
-            scores = dot(kv, w_q[slot])
+            scores = dot(kv, w_q[...])
             row_ix = offset + key_chunk - TAIL + lax.broadcasted_iota(jnp.int32, (TAIL, q_block), 0)
             tail = jnp.where(row_ix < count_ref[pl.ds(owner, 1), :q_block], scores[key_chunk - TAIL:, :], NEG_FILL)
             scores = jnp.concatenate([scores[:key_chunk - TAIL, :], tail], axis=0)
             prob = jnp.exp2(scores * factor - lse_buf[unit])
-            p_buf[slot] = prob.astype(BF16)
-            ds_buf[slot] = (prob * (dot(kv, w_do[slot]) - delta_buf[unit])).astype(BF16)
-
-        def second_stage(step):
-            group, owner, offset, rows, unit, slot = place_of(step)
-            d_scores = ds_buf[slot]
+            p_buf[...] = prob.astype(BF16)
+            ds_buf[...] = (prob * (dot(kv, w_do[...]) - delta_buf[unit])).astype(BF16)
+
+        def second_stage(step, parity):
+            w_q, w_do, p_buf, ds_buf = buffers[parity]
+            group, owner, offset, rows, unit = place_of(step)
+            d_scores = ds_buf[...]
             spot = pl.ds(pl.multiple_of(offset, key_chunk), key_chunk)
-            dkv_acc[group, spot, :] += dot(d_scores, w_q[slot], NT) + dot(p_buf[slot], w_do[slot], NT)
+            dkv_acc[group, spot, :] += dot(d_scores, w_q[...], NT) + dot(p_buf[...], w_do[...], NT)
             dq_acc[unit] += dot(kvt_ref[:head_dim, rows], d_scores)
 
         def exchange(step):
@@ -621,16 +617,22 @@
         done = (steps - 1) // FINAL_STEPS - FINAL_LAG + 1
         assert (steps - 1) % FINAL_STEPS >= 1 and 0 < done < total - 2 and HOLD_STEP > 2 * per_group + 2 and HOLD_STEP % 4 == 0
 
-        first_stage(0)
-
-        def body(step, carry):
-            exchange(step)
-            second_stage(step - 1)
-            first_stage(step)
+        first_stage(0, 0)
+
+        def body(pair, carry):
+            for parity in (1, 0):
+                step = 2 * pair + 2 - parity
+                exchange(step)
+                second_stage(step - 1, 1 - parity)
+                first_stage(step, parity)
             return carry
 
-        lax.fori_loop(1, steps, body, 0)
-        second_stage(steps - 1)
+        assert steps % 2 == 0
+        lax.fori_loop(0, steps // 2 - 1, body, 0)
+        exchange(steps - 1)
+        first_stage(steps - 1, 1)
+        second_stage(steps - 2, 0)
+        second_stage(steps - 1, 1)
 
         def gather_dq(unit, carry):
             head, rows, cols = unit_spots(unit)
@@ -640,24 +642,31 @@
         lax.fori_loop(0, units, gather_dq, 0)
         last = total - 1
         local[last] = dot(dq_all[...], hid_ref[...]).T
+        mate_copy(last).start()
         dkv_copies[2].wait_recv()
         dkv_copies[1].wait_recv()
         dkv = dkv_acc[3] + dkv_in[2] + dkv_in[1]
         lane = lax.broadcasted_iota(jnp.int32, dkv.shape, 1)
         dkv = jnp.where(lane < head_dim, dkv * scale, dkv).astype(BF16)
-        mate_copy(last).start()
         kv_local[...] = dot(dkv, hid_ref[...], TN)
-        dx_acc[...] += dot(dkv, jnp.concatenate([w_kt_ref[...], w_vt_ref[...]], axis=0))
+        d_agg = dot(dpre_buf[...], w_msg_ref[...], NT).astype(BF16)
+        halo_out[...] = dot(adj_ref[part_rows:, :], d_agg).astype(BF16).reshape(halo_out.shape)
         kv_to_mate.start()
         chip_sum(last)
+        dx_acc[...] = 2.0 * dz_buf[...].astype(F32) + dot(dpre_buf[...], w_self_ref[...], NT)
+        for peer in (mate, cross, other):
+            halo_copy(peer, me).start()
+        halo_in[me] = halo_out[me]
+        cross_copy(last).start()
         kv_to_mate.wait_recv()
         kv_own[0] = kv_local[pl.ds(pl.multiple_of(side * kv_half, kv_half), kv_half), :] + kv_in[0]
+        dx_acc[...] += dot(adj_ref[:part_rows, :], d_agg)
+        kv_to_cross.start()
+        dx_acc[...] += dot(dkv, jnp.concatenate([w_kt_ref[...], w_vt_ref[...]], axis=0))
         for peer in (mate, cross, other):
             halo_copy(me, peer).wait_recv()
         slot_hot = jnp.where(lax.broadcasted_iota(jnp.int32, (part_rows, 4 * halo_pair), 0) == slot_ref[...], 1.0, 0.0).astype(BF16)
         dx_acc[...] += dot(slot_hot, halo_in[...].reshape(4 * halo_pair, width))
-        cross_copy(last).start()
-        kv_to_cross.start()
         dx_ref[...] = (dx_acc[...] + dot(dq_all[...], w_q_ref[...].T, TN)).astype(BF16)
         for index in range(done, total):
             group_sum(index)
@@ -675,12 +684,10 @@
 
     pl.run_scoped(
         attention_phase,
-        pltpu.VMEM((2, 2 * head_dim, q_block), BF16),
-        pltpu.VMEM((2, 2 * head_dim, q_block), BF16),
+        *[pltpu.VMEM((2 * head_dim, q_block), BF16)] * 4,
+        *[pltpu.VMEM((key_chunk, q_block), BF16)] * 4,
         pltpu.VMEM((units, 1, q_block), F32),
         pltpu.VMEM((units, 1, q_block), F32),
-        pltpu.VMEM((2, key_chunk, q_block), BF16),
-        pltpu.VMEM((2, key_chunk, q_block), BF16),
         pltpu.VMEM((units, head_dim, q_block), F32),
         pltpu.VMEM((width, part_rows), BF16),
         pltpu.VMEM((4, part_rows, 2 * head_dim), F32),

time: 281 us -> 279 us (level)
  no operation moved by 1% of the time
where the time goes in v5:
time: 279 us
  Pallas kernels  278 us (100%)
    pallas_call x1, Pallas kernels, backward(): pl.pallas_call(functools.partial(backward_kernel, head_dim, q_block, key_...  173 us
    pallas_call x1, Pallas kernels, front(): pl.pallas_call(functools.partial(front_kernel, head_dim), out_shape=[jax....  94.3 us
    pallas_call x1, Pallas kernels, finish(): pl.pallas_call(functools.partial(finish_kernel, plan), out_shape=shapes,...  11.1 us

profile of v5, /device:TPU:0, one launch (start us, length us, event | category | flops | bytes accessed | tf_op | source)
XLA Modules:
  0.0 278.8 jit_solution(9090507724448030008)
XLA Ops:
  0.6 94.3 %front.1 = (bf16[512,1024]{1,0:T(8,128)(2,1)}, f32[8,1024]{1,0:T(8,128)}, s32[1,128]{1,0:T(1,128)}, s32[4,512]{1,0:T(4,128)}, bf16[512,1024]{1,0:T(8,128)(2,1)},...) custom-call(s32[1,1024]{1,0:T(1,128)} %bitcast.13, ...), custom_call_target="tpu_custom_call" | custom-call | flops 25769803776 | bytes 20971520 | tf_op jit(solution)/shard_map/front/pallas_call | solution.py:242
  95.0 172.6 %backward.1 = (bf16[1024,512]{1,0:T(8,128)(2,1)}, bf16[1024,512]{1,0:T(8,128)(2,1)}, f32[512,2048]{1,0:T(8,128)}, f32[2048,512]{1,0:T(8,128)}, f32[512,512]{1,0:...) custom-call(s32[4,512]{1,0:T(4,128)} %get-tuple-element.40.count_ref, ...), custom_call_target="tpu_custom_call" | custom-call | flops 21474836480 | bytes 41943040 | tf_op jit(solution)/shard_map/backward/pallas_call | solution.py:724
  267.6 11.1 %finish.1 = (bf16[1024,512]{1,0:T(8,128)(2,1)}, bf16[1024,512]{1,0:T(8,128)(2,1)}, f32[512,2048]{1,0:T(8,128)}, f32[2048,512]{1,0:T(8,128)}, f32[512,512]{1,0:T(...) custom-call(bf16[1024,512]{1,0:T(8,128)(2,1)} %get-tuple-element.51., ...), custom_call_target="tpu_custom_call" | custom-call | flops 1048576 | bytes 31457280 | tf_op jit(solution)/shard_map/finish/pallas_call | solution.py:784

commit v6 on v5

--- a/solution.py
+++ b/solution.py
@@ -178,7 +178,6 @@
 
     hid_ref[...] = (x_ref[...].astype(F32) + pos_acc[...]).astype(BF16)
     kv_all[me] = dot(hid_ref[...], jnp.concatenate([w_kt_ref[...], w_vt_ref[...]], axis=0), NT).astype(BF16)
-    q_ref[...] = dot(w_q_ref[...].T, hid_ref[...], NT).astype(BF16)
     kv_piece = rows_dev // KV_PIECES
 
     def kv_copy(owner, k, kind, peer):
@@ -188,8 +187,6 @@
     kv_to_cross = [kv_copy(me, k, 0, cross) for k in range(KV_PIECES)]
     kv_to_mate = [kv_copy(me, k, 1, mate) for k in range(KV_PIECES)]
     kv_relay = [kv_copy(cross, k, 2, mate) for k in range(KV_PIECES)]
-    for copy in kv_to_cross + kv_to_mate:
-        copy.start()
     size = kv_all.shape[2]
     eye = jnp.where(lax.broadcasted_iota(jnp.int32, (size, size), 0) == lax.broadcasted_iota(jnp.int32, (size, size), 1), 1.0, 0.0).astype(BF16)
 
@@ -198,11 +195,14 @@
         kv_ref[rows, :] = kv_all[owner]
         kvt_ref[:, rows] = dot(eye, kv_all[owner], NT).astype(BF16)
 
+    keep_kv(me)
+    for copy in kv_to_cross + kv_to_mate:
+        copy.start()
+    q_ref[...] = dot(w_q_ref[...].T, hid_ref[...], NT).astype(BF16)
     for peer in peers:
         halo_copy(me, peer).wait_recv()
     agg = dot(adj_ref[:rows_dev, :], x_ref[...], TN) + dot(adj_ref[rows_dev:, :], halo_in[...].reshape(nodes * halo_pair, width), TN)
     agg_ref[...] = agg.astype(BF16)
-    keep_kv(me)
     kv_to_cross[0].wait_recv()
     kv_relay[0].start()
     pre_ref[...] = dot(agg_ref[...], w_msg_ref[...]) + dot(x_ref[...], w_self_ref[...])

time: 279 us -> 279 us (level)
  no operation moved by 1% of the time
where the time goes in v6:
time: 279 us
  Pallas kernels  278 us (100%)
    pallas_call x1, Pallas kernels, backward(): pl.pallas_call(functools.partial(backward_kernel, head_dim, q_block, key_...  172 us
    pallas_call x1, Pallas kernels, front(): pl.pallas_call(functools.partial(front_kernel, head_dim), out_shape=[jax....  94.3 us
    pallas_call x1, Pallas kernels, finish(): pl.pallas_call(functools.partial(finish_kernel, plan), out_shape=shapes,...  11.1 us

profile of v6, /device:TPU:0, one launch (start us, length us, event | category | flops | bytes accessed | tf_op | source)
XLA Modules:
  0.0 278.7 jit_solution(5907212871855301907)
XLA Ops:
  0.6 94.3 %front.1 = (bf16[512,1024]{1,0:T(8,128)(2,1)}, f32[8,1024]{1,0:T(8,128)}, s32[1,128]{1,0:T(1,128)}, s32[4,512]{1,0:T(4,128)}, bf16[512,1024]{1,0:T(8,128)(2,1)},...) custom-call(s32[1,1024]{1,0:T(1,128)} %bitcast.13, ...), custom_call_target="tpu_custom_call" | custom-call | flops 25769803776 | bytes 20971520 | tf_op jit(solution)/shard_map/front/pallas_call | solution.py:242
  94.9 172.5 %backward.1 = (bf16[1024,512]{1,0:T(8,128)(2,1)}, bf16[1024,512]{1,0:T(8,128)(2,1)}, f32[512,2048]{1,0:T(8,128)}, f32[2048,512]{1,0:T(8,128)}, f32[512,512]{1,0:...) custom-call(s32[4,512]{1,0:T(4,128)} %get-tuple-element.40.count_ref, ...), custom_call_target="tpu_custom_call" | custom-call | flops 21474836480 | bytes 41943040 | tf_op jit(solution)/shard_map/backward/pallas_call | solution.py:724
  267.4 11.1 %finish.1 = (bf16[1024,512]{1,0:T(8,128)(2,1)}, bf16[1024,512]{1,0:T(8,128)(2,1)}, f32[512,2048]{1,0:T(8,128)}, f32[2048,512]{1,0:T(8,128)}, f32[512,512]{1,0:T(...) custom-call(bf16[1024,512]{1,0:T(8,128)(2,1)} %get-tuple-element.51., ...), custom_call_target="tpu_custom_call" | custom-call | flops 1048576 | bytes 31457280 | tf_op jit(solution)/shard_map/finish/pallas_call | solution.py:784
